TPU v7x, 32 devices: a whole 2x2x4 slice. The times are simulated.
32 devices in a mesh: dom: 16 (over z, y, x), mp: 2 (over core).
Axes of the slice: x: 2, y: 2, z: 4, core: 2. Of those that a mesh axis runs over, the one named last changes fastest.
Arguments:
- table: bfloat16 [65536, 768], P('dom', 'mp'), may hold values from -6 to 6
- weight_a: bfloat16 [1536, 512], P(None, 'mp'), may hold values from -0.15625 to 0.15625
- bias_a: float32 [512], replicated, may hold values from -3 to 3
- weight_b: bfloat16 [1024, 512], P(None, 'mp'), may hold values from -0.25 to 0.25
- bias_b: float32 [512], replicated, may hold values from -3 to 3
- requests: int32 [16, 16, 128], P('dom'), may hold values from 0 to 4095
- near_a: int32 [16384, 10], P('dom'), may hold values from 0 to 2047
- self_a: int32 [16384], P('dom'), may hold values from 0 to 2047
- count_a: int32 [16384], P('dom'), may hold values from 1 to 10
- near_b: int32 [4096, 5], P('dom'), may hold values from 0 to 1023
- self_b: int32 [4096], P('dom'), may hold values from 0 to 1023
- count_b: int32 [4096], P('dom'), may hold values from 1 to 5
Outputs:
- embedding: bfloat16 [4096, 512], P('dom', 'mp')
Inputs may be any that keep to these rules, and one draw needn't show every extreme that they name: `requests`: local row indices at the owner. `near_a`: slots of the same minibatch; entries at j >= count_a are padding. `near_b`: positions within the same minibatch; entries at j >= count_b are padding.
All inputs are finite; a program needn't handle non-finite values.
Results may differ from a plain program's by a relative error of at most 0.0074.
Values may be sent and summed in bfloat16 or wider, within the bound.
No kernel may reach another device: no remote copies, remote signals or barrier semaphores. Data moves between devices by JAX's collectives and lax.ppermute only.
A program may use at most 64 MiB of HBM per device.

v0:
```python
import jax
import jax.numpy as jnp
from jax import lax
from jax.sharding import PartitionSpec as P

F = 768
H = 512


def mean_rows(source, neighbours, counts):
    total_rows = neighbours.shape[0]
    fanout = neighbours.shape[1]
    block = min(512, total_rows)
    columns = lax.broadcasted_iota(jnp.int32, (1, source.shape[0]), 1)

    def one_block(pieces):
        near, valid = pieces
        weights = jnp.zeros((block, source.shape[0]), jnp.bfloat16)
        for column in range(fanout):
            picked = (near[:, column : column + 1] == columns) & (valid[:, None] > column)
            weights = weights + picked.astype(jnp.bfloat16)
        total = jnp.dot(weights, source, preferred_element_type=jnp.float32)
        return (total / valid[:, None].astype(jnp.float32)).astype(jnp.bfloat16)

    result = lax.map(one_block, (neighbours.reshape(-1, block, fanout), counts.reshape(-1, block)))
    return result.reshape(total_rows, source.shape[1])


def shards(
    table,
    weight_a,
    bias_a,
    weight_b,
    bias_b,
    requests,
    near_a,
    self_a,
    count_a,
    near_b,
    self_b,
    count_b,
):
    half_hidden = weight_a.shape[1]
    half_feature = table.shape[1]
    mp_index = lax.axis_index("mp")
    asked = requests[0]
    found = table[lax.all_to_all(asked, "dom", split_axis=0, concat_axis=0, tiled=True)]
    fetched = lax.all_to_all(found, "dom", split_axis=0, concat_axis=0, tiled=True)
    fetched = fetched.reshape(-1, half_feature)
    own_rows = fetched[self_a]
    mean_a = mean_rows(fetched, near_a, count_a)
    whole_a = lax.all_gather(weight_a, "mp", axis=1, tiled=True)
    own_weight = lax.dynamic_slice_in_dim(whole_a, mp_index * half_feature, half_feature, 0)
    near_weight = lax.dynamic_slice_in_dim(whole_a, F + mp_index * half_feature, half_feature, 0)
    partial_value = jnp.dot(own_rows, own_weight, preferred_element_type=jnp.float32)
    partial_value = partial_value + jnp.dot(mean_a, near_weight, preferred_element_type=jnp.float32)
    bias_part = lax.dynamic_slice_in_dim(bias_a, mp_index * half_hidden, half_hidden, 0)
    before = lax.psum_scatter(partial_value, "mp", scatter_dimension=1, tiled=True) + bias_part
    hidden_a = jax.nn.relu(before).astype(jnp.bfloat16)
    bias_part = lax.dynamic_slice_in_dim(bias_b, mp_index * half_hidden, half_hidden, 0)
    mean_b = mean_rows(hidden_a, near_b, count_b)
    own_b = lax.all_gather(hidden_a[self_b], "mp", axis=1, tiled=True)
    mean_whole = lax.all_gather(mean_b, "mp", axis=1, tiled=True)
    inputs_b = jnp.concatenate([own_b, mean_whole], axis=1)
    state = jax.nn.relu(jnp.dot(inputs_b, weight_b, preferred_element_type=jnp.float32) + bias_part)
    squares = lax.psum(jnp.sum(state * state, axis=1), "mp")
    scaled = state * jnp.sqrt(jnp.float32(H)) / jnp.sqrt(squares[:, None] + H)
    return scaled.astype(jnp.bfloat16)


def solution(mesh):
    placed = (
        P("dom", "mp"),
        P(None, "mp"),
        P(),
        P(None, "mp"),
        P(),
        P("dom", None, None),
        P("dom", None),
        P("dom"),
        P("dom"),
        P("dom", None),
        P("dom"),
        P("dom"),
    )
    return jax.shard_map(
        shards, mesh=mesh, in_specs=placed, out_specs=P("dom", "mp"), check_vma=False
    )
```

profile of v0, /device:TPU:0, one launch (start us, length us, event | category | flops | bytes accessed | tf_op | source)
XLA Modules:
  0.0 135.9 jit_solution(11270580848167446451)
XLA Ops:
  6.5 15.8 %all_to_all.17 = s32[16,1,128]{2,1,0:T(1,128)S(1)} all-to-all(s32[16,1,128]{2,1,0:T(1,128)} %bitcast.82), channel_id=1, replica_groups=mesh['dom'=16,'mp'=2] {'dom'}, dimensions={0} | all-to-all | bytes 16384 | tf_op jit(solution)/shard_map/all_to_all | solution.py:47
  22.4 9.0 %gather_fusion = bf16[2048,384]{1,0:T(8,128)(2,1)} fusion(bf16[4096,384]{1,0:T(8,128)(2,1)S(1)} %copy-done, s32[2048]{0:T(1024)S(1)} %fusion.112), kind=kCustom, calls=%fused_computation | custom fusion | bytes 3153920 | tf_op jit(solution)/shard_map/gather | solution.py:47
  31.4 4.5 %all-to-all-start.1 = ((bf16[16,128,384]{2,1,0:T(8,128)(2,1)}), bf16[16,128,384]{2,1,0:T(8,128)(2,1)}, u32[]{:S(2)}, u32[]{:S(2)}) async-start(bf16[16,128,384]{2,1,0:T(8,128)(2,1)} %bitcast.67), calls=%async_computation.1 | async-start | bytes 3145728 | tf_op jit(solution)/shard_map/all_to_all | solution.py:48
  36.0 0.7 all-gather.3.cloned.1.call-update
  36.9 32.3 %all-to-all-done.1 = bf16[16,128,384]{2,1,0:T(8,128)(2,1)} async-done(((bf16[16,128,384]{2,1,0:T(8,128)(2,1)}), bf16[16,128,384]{2,1,0:T(8,128)(2,1)}, u32[]{:S(2)}, u32[]{:S(2)}) %all-to-all-start.1) | async-done | bytes 1572896 | tf_op jit(solution)/shard_map/all_to_all | solution.py:48
  69.2 22.4 %while.16 = (s32[]{:T(128)}, bf16[2,512,384]{2,1,0:T(8,128)(2,1)}, s32[2,512,10]{1,0,2:T(2,128)S(1)}, s32[2,512]{1,0:T(2,128)S(1)}, bf16[2048,384]{1,0:T(8,128)(2,1)}, /*index=5*/s32[]{:T(128)}) while((s32[]{:T(128)}, bf16[2,512,384]{2,1,0:T(8,128)(2,1)}, s32[2,512,10]{1,0,2:T(2,128)S(1)}, s32[2,512]{1,0:T(2,128)S(1)}, ...), condition=%wide.region_1.2_spmd.clone.clone, body=%wide.region_0.1_spmd.clone.clone.sunk | while | flops 858134016 | bytes 2130009 | solution.py:25
  69.2 0.1 compare_reduce_fusion.11
  69.3 11.0 %fusion.134 = bf16[2,512,384]{2,1,0:T(8,128)(2,1)} fusion(bf16[2,512,384]{2,1,0:T(8,128)(2,1)} %get-tuple-element.255, s32[]{:T(128)S(6)} %copy.27, bf16[2048,384]{1,0:T(8,128)(2,1)} %get-tuple-element.264, s32[512]{0:T(512)S(1)} %bitcast.71, s32[512]{0:T(512)S(1)} %bitcast.72, s32[512]{0:T(512)S(1)} %bitcast.73, s32[512]{0:T(512)S(1)} %bitcast.74, ...), kind=kOutput, calls=%fused_computation.67.clone.1 | convolution fusion | flops 858128384 | bytes 1993732 | tf_op jit(solution)/shard_map/while/body/eval_jaxpr/dot_general | solution.py:22
  80.4 0.1 compare_reduce_fusion.11
  80.5 11.0 %fusion.134 = bf16[2,512,384]{2,1,0:T(8,128)(2,1)} fusion(bf16[2,512,384]{2,1,0:T(8,128)(2,1)} %get-tuple-element.255, s32[]{:T(128)S(6)} %copy.27, bf16[2048,384]{1,0:T(8,128)(2,1)} %get-tuple-element.264, s32[512]{0:T(512)S(1)} %bitcast.71, s32[512]{0:T(512)S(1)} %bitcast.72, s32[512]{0:T(512)S(1)} %bitcast.73, s32[512]{0:T(512)S(1)} %bitcast.74, ...), kind=kOutput, calls=%fused_computation.67.clone.1 | convolution fusion | flops 858128384 | bytes 1993732 | tf_op jit(solution)/shard_map/while/body/eval_jaxpr/dot_general | solution.py:22
  91.6 6.4 %gather_fusion.1 = bf16[1024,384]{1,0:T(8,128)(2,1)} fusion(bf16[2048,384]{1,0:T(8,128)(2,1)} %bitcast.4, s32[1024]{0:T(1024)S(1)} %fusion.113), kind=kCustom, calls=%fused_computation.1 | custom fusion | bytes 1576960 | tf_op jit(solution)/shard_map/gather | solution.py:50
  98.0 2.0 %fusion.109 = f32[1024,512]{1,0:T(8,128)S(1)} fusion(bf16[1024,384]{1,0:T(8,128)(2,1)} %gather_fusion.1, bf16[1536,512]{1,0:T(8,128)(2,1)} %all-gather.3.cloned.1.call-done, s32[]{:T(128)S(6)} %select_n.28), kind=kOutput, calls=%fused_computation.120 | convolution fusion | flops 402653184 | bytes 3276804 | tf_op jit(solution)/shard_map/dot_general | solution.py:55
  100.1 3.0 %convolution_add_fusion = f32[1024,512]{1,0:T(8,128)} fusion(f32[1024,512]{1,0:T(8,128)S(1)} %fusion.109, bf16[1024,384]{1,0:T(8,128)(2,1)S(1)} %bitcast.69, bf16[1536,512]{1,0:T(8,128)(2,1)} %all-gather.3.cloned.1.call-done, s32[]{:T(128)S(6)} %select_n.29), kind=kOutput, calls=%fused_computation.81 | convolution fusion | flops 403177472 | bytes 5373956 | tf_op jit(solution)/shard_map/dot_general | solution.py:56
  103.2 0.1 dynamic_slice.28
  103.2 0.1 dynamic_slice.29
  103.4 11.2 %reduce-scatter.2.cloned.1.call-done = f32[1024,256]{1,0:T(8,128)} async-done(((f32[1024,512]{1,0:T(8,128)}), f32[1024,256]{1,0:T(8,128)}) %reduce-scatter.2.cloned.1.call-update) | async-done | bytes 1048592 | tf_op jit(solution)/shard_map/reduce_scatter | solution.py:58
  114.6 2.1 %maximum_convert_fusion = bf16[1024,256]{1,0:T(8,128)(2,1)} fusion(f32[1024,256]{1,0:T(8,128)} %reduce-scatter.2.cloned.1.call-done, f32[256]{0:T(256)S(1)} %dynamic_slice.28), kind=kLoop, calls=%fused_computation.91 | loop fusion | flops 786432 | bytes 1573888 | tf_op jit(solution)/shard_map/convert_element_type | solution.py:59
  116.7 2.1 %gather_fusion.2 = bf16[256,256]{1,0:T(8,128)(2,1)S(1)} fusion(bf16[1024,256]{1,0:T(8,128)(2,1)} %maximum_convert_fusion, s32[1024]{0:T(1024)S(1)} %pad_clamp_fusion), kind=kCustom, calls=%fused_computation.2 | custom fusion | bytes 263168 | tf_op jit(solution)/shard_map/gather | solution.py:62
  118.8 2.1 %all-gather = bf16[256,512]{1,0:T(8,128)(2,1)S(1)} all-gather(bf16[256,256]{1,0:T(8,128)(2,1)S(1)} %gather_fusion.2), channel_id=2, replica_groups=mesh['dom'=16,'mp'=2] {'mp'}, dimensions={1}, use_global_device_ids=true | all-gather | bytes 393216 | tf_op jit(solution)/shard_map/all_gather | solution.py:62
  121.0 2.5 %fusion.75 = bf16[256,256]{1,0:T(8,128)(2,1)S(1)} fusion(bf16[1024,256]{1,0:T(8,128)(2,1)} %maximum_convert_fusion, s32[256]{0:T(256)S(1)} %bitcast.86, s32[256]{0:T(256)S(1)} %bitcast.87, s32[256]{0:T(256)S(1)} %bitcast.84, s32[256]{0:T(256)S(1)} %bitcast.85, s32[256]{0:T(256)S(1)} %bitcast.83, pred[256]{0:T(512)(128)(4,1)S(1)} %get-tuple-element.170, ...), kind=kOutput, calls=%fused_computation.85 | convolution fusion | flops 140902400 | bytes 662784 | tf_op jit(solution)/shard_map/while/body/eval_jaxpr/dot_general | solution.py:22
  123.4 2.0 %all_gather.11 = bf16[256,512]{1,0:T(8,128)(2,1)S(1)} all-gather(bf16[256,256]{1,0:T(8,128)(2,1)S(1)} %fusion.75), channel_id=1, replica_groups=mesh['dom'=16,'mp'=2] {'mp'}, dimensions={1}, use_global_device_ids=true | all-gather | bytes 393216 | tf_op jit(solution)/shard_map/all_gather | solution.py:63
  125.4 0.4 multiply_reduce_fusion
  125.8 2.5 %psum.7 = f32[256]{0:T(256)S(1)} all-reduce(f32[256]{0:T(256)S(1)} %get-tuple-element.171), channel_id=1, replica_groups=mesh['dom'=16,'mp'=2] {'mp'}, use_global_device_ids=true, to_apply=%region_4.5 | all-reduce | flops 256 | bytes 2048 | tf_op jit(solution)/shard_map/psum | solution.py:66
  128.3 0.8 copy.18
  (46 shorter events, 0.4 us)
Async XLA Ops:
  6.5 15.8 %copy-start = (bf16[4096,384]{1,0:T(8,128)(2,1)S(1)}, bf16[4096,384]{1,0:T(8,128)(2,1)}, u32[]{:S(2)}) copy-start(bf16[4096,384]{1,0:T(8,128)(2,1)} %param.14) | copy-start | bytes 9437188
  31.4 5.3 %copy-start.4 = (s32[1024]{0:T(1024)S(1)}, s32[1024]{0:T(1024)}, u32[]{:S(2)}) copy-start(s32[1024]{0:T(1024)} %param.22) | copy-start | bytes 12292
  31.4 5.4 %copy-start.2 = (s32[1024,10]{0,1:T(8,128)S(1)}, s32[1024,10]{0,1:T(8,128)}, u32[]{:S(2)}) copy-start(s32[1024,10]{0,1:T(8,128)} %param.20) | copy-start | bytes 122884
  31.4 5.4 %copy-start.5 = (s32[1024]{0:T(1024)S(1)}, s32[1024]{0:T(1024)}, u32[]{:S(2)}) copy-start(s32[1024]{0:T(1024)} %param.21) | copy-start | bytes 12292
  31.4 37.8 %all-to-all-start.1 = ((bf16[16,128,384]{2,1,0:T(8,128)(2,1)}), bf16[16,128,384]{2,1,0:T(8,128)(2,1)}, u32[]{:S(2)}, u32[]{:S(2)}) async-start(bf16[16,128,384]{2,1,0:T(8,128)(2,1)} %bitcast.67), calls=%async_computation.1 | async-start | bytes 3145728 | tf_op jit(solution)/shard_map/all_to_all | solution.py:48
  36.0 62.1 %all-gather.3.cloned.1.call-start = ((), (), s32[]{:S(2)}) async-start(), calls=%async_computation.3 | async-start | bytes 2359296 | tf_op jit(solution)/shard_map/all_gather | solution.py:52
  36.7 77.9 %reduce-scatter.2.cloned.1.call-start = ((), (), s32[]{:S(2)}) async-start(), calls=%async_computation.4 | async-start | bytes 3145728 | tf_op jit(solution)/shard_map/reduce_scatter | solution.py:58
  98.0 2.0 %copy-start.1 = (bf16[2,512,384]{2,1,0:T(8,128)(2,1)S(1)}, bf16[2,512,384]{2,1,0:T(8,128)(2,1)}, u32[]{:S(2)}) copy-start(bf16[2,512,384]{2,1,0:T(8,128)(2,1)} %get-tuple-element.82) | copy-start | bytes 2359300
  100.0 3.1 %copy-start.8 = (f32[512]{0:T(512)S(1)}, f32[512]{0:T(512)}, u32[]{:S(2)}) copy-start(f32[512]{0:T(512)} %param.16) | copy-start | bytes 6148
  100.1 3.2 %copy-start.9 = (f32[512]{0:T(512)S(1)}, f32[512]{0:T(512)}, u32[]{:S(2)}) copy-start(f32[512]{0:T(512)} %param.18) | copy-start | bytes 6148
  100.1 3.3 %copy-start.3 = (s32[256]{0:T(256)S(1)}, s32[256]{0:T(256)}, u32[]{:S(2)}) copy-start(s32[256]{0:T(256)} %param.25) | copy-start | bytes 3076
  100.1 3.2 %copy-start.7 = (s32[256]{0:T(256)S(1)}, s32[256]{0:T(256)}, u32[]{:S(2)}) copy-start(s32[256]{0:T(256)} %param.24) | copy-start | bytes 3076
  100.1 3.3 %copy-start.6 = (s32[256,5]{0,1:T(8,128)S(1)}, s32[256,5]{0,1:T(8,128)}, u32[]{:S(2)}) copy-start(s32[256,5]{0,1:T(8,128)} %param.23) | copy-start | bytes 15364
  118.8 6.6 %copy-start.10 = (bf16[1024,256]{1,0:T(8,128)(2,1)S(1)}, bf16[1024,256]{1,0:T(8,128)(2,1)}, u32[]{:S(2)}) copy-start(bf16[1024,256]{1,0:T(8,128)(2,1)} %param.17) | copy-start | bytes 1572868
Sparse Core Ops, SparseCore 0:
  38.3 10.6 all-gather.2
  103.3 11.2 reduce-scatter.1
where the time goes:
time: 136 us
  waiting for transfers between devices  44.3 us (33%)
  matrix products  30 us (22%)
  blocking collectives  22.4 us (16%)
  local copies, waits for them, and re-layouts  18.7 us (14%)
  between operations  13.6 us (10%)
  starting transfers between devices  4.61 us (3%)
  other arithmetic  2.36 us (2%)
    all_to_all x1, waiting for transfers between devices, shards(): lax.all_to_all(found, 'dom', split_axis=0, concat_axis=0, tiled=True)  32.3 us
    dot_general x3, matrix products, one_block(): total = jnp.dot(weights, source, preferred_element_type=jnp.float32)  24.6 us
    all_to_all x1, blocking collectives, shards(): lax.all_to_all(asked, 'dom', split_axis=0, concat_axis=0, tiled=True)  15.8 us
    reduce_scatter x1, waiting for transfers between devices, shards(): lax.psum_scatter(partial_value, 'mp', scatter_dimension=1, tiled=True)  11.2 us
    gather x1, local copies, waits for them, and re-layouts, shards(): table[lax.all_to_all(asked, 'dom', split_axis=0, concat_axis=0, tiled=True)]  9.04 us
    gather x1, local copies, waits for them, and re-layouts, shards(): own_rows = fetched[self_a]  6.45 us
    all_to_all x1, starting transfers between devices, shards(): lax.all_to_all(found, 'dom', split_axis=0, concat_axis=0, tiled=True)  4.53 us
    dot_general x1, matrix products, shards(): jnp.dot(mean_a, near_weight, preferred_element_type=jnp.float32)  3.02 us
  transfers between devices with their start and end apart: 3, of which 2 were waited for; matrix products, arithmetic and copies ran while one was open for 21% of the time, Pallas kernels for 0%

commit v1 on v0

v1 whole, which is shorter than its diff:
```python
import functools

import jax
import jax.numpy as jnp
from jax import lax
from jax.experimental import pallas as pl
from jax.sharding import PartitionSpec as P


LANES = 128
ROWS = 32


def spans_of(per):
    return ((0, per),)


def split_index(value, size):
    if size & (size - 1) == 0:
        return lax.shift_right_logical(value, size.bit_length() - 1), value & (size - 1)
    quotient = lax.div(value, size)
    return quotient, value - quotient * size


def place_of(slots, per, owners, spans):
    owner, row = split_index(slots, per)
    place = jnp.zeros_like(slots)
    for low, high in spans:
        inside = (row >= low) & (row < high)
        place = jnp.where(inside, owners * low + owner * (high - low) + row - low, place)
    return place


def fill_counts(tab_ref, fan, place_fn, outs):
    total = tab_ref.shape[0]
    bits = max(1, fan.bit_length())
    fields = 32 // bits
    blocks = [(ref, at) for ref in outs for at in range(ref.shape[2] // LANES)]
    words = -(-len(blocks) // fields)
    rows = min(ROWS, total)
    lanes = lax.broadcasted_iota(jnp.int32, (rows, LANES), 1)
    column = lax.broadcasted_iota(jnp.int32, (rows, fan + 1), 1)

    def step(index, carry):
        at = pl.multiple_of(index * rows, rows)
        here = pl.ds(at, rows)
        piece = tab_ref[here, :]
        place = place_fn(piece[:, : fan + 1])
        block, low = split_index(place, LANES)
        valid = column < piece[:, fan + 1 : fan + 2]
        word, field = split_index(block, fields)
        unit = jnp.where(valid, jnp.left_shift(jnp.ones_like(field), field * bits), 0)
        units = [jnp.where(word == w, unit, 0) for w in range(words)]
        sums = [jnp.zeros((rows, LANES), jnp.int32) for _ in range(words)]
        for j in range(fan):
            hit = lanes == low[:, j : j + 1]
            for w in range(words):
                sums[w] = sums[w] + jnp.where(hit, units[w][:, j : j + 1], 0)
        own = place[:, fan : fan + 1]
        for number, (ref, part) in enumerate(blocks):
            count = lax.shift_right_logical(sums[number // fields], bits * (number % fields))
            count = (count & ((1 << bits) - 1)).astype(jnp.float32)
            cols = slice(part * LANES, (part + 1) * LANES)
            ref[0, here, cols] = count.astype(jnp.bfloat16)
            one = jnp.where(lanes + number * LANES == own, 1.0, 0.0)
            ref[1, here, cols] = one.astype(jnp.bfloat16)
        return carry

    lax.fori_loop(0, total // rows, step, 0)


def count_matrices(tab, fan, place_fn, widths):
    total = tab.shape[0]

    def body(tab_ref, *outs):
        fill_counts(tab_ref, fan, place_fn, outs)

    return pl.pallas_call(
        body,
        out_shape=[jax.ShapeDtypeStruct((2, total, width), jnp.bfloat16) for width in widths],
        cost_estimate=pl.CostEstimate(flops=10**9, bytes_accessed=10**7, transcendentals=0),
    )(tab)


def gather_sums(counts, rows, before):
    hops = counts.shape[1]
    width = counts.shape[2]
    cols = rows.shape[1]
    block = min(256, hops)

    def body(*refs):
        c_ref, x_ref = refs[0], refs[1]
        o_ref = refs[-1]
        value = jnp.dot(c_ref[...].reshape(2 * block, width), x_ref[...], preferred_element_type=jnp.float32)
        if before is not None:
            value = value + refs[2][...].reshape(2 * block, cols)
        o_ref[...] = value.reshape(2, block, cols)

    acc_spec = pl.BlockSpec((2, block, cols), lambda i: (0, i, 0))
    specs = [pl.BlockSpec((2, block, width), lambda i: (0, i, 0)), pl.BlockSpec((width, cols), lambda i: (0, 0))]
    operands = [counts, rows]
    if before is not None:
        specs.append(acc_spec)
        operands.append(before)
    return pl.pallas_call(
        body,
        grid=(hops // block,),
        in_specs=specs,
        out_specs=acc_spec,
        out_shape=jax.ShapeDtypeStruct((2, hops, cols), jnp.float32),
        cost_estimate=pl.CostEstimate(flops=4 * hops * width * cols, bytes_accessed=10**7, transcendentals=0),
        name="gather_sums",
    )(*operands)


def first_layer(counts, rows, before, count_a, weight):
    hops = counts.shape[1]
    width = counts.shape[2]
    cols = rows.shape[1]
    hidden = weight.shape[2]
    block = min(256, hops)

    def body(*refs):
        c_ref, x_ref, n_ref, w_ref = refs[:4]
        o_ref, s_ref = refs[-2:]
        value = jnp.dot(c_ref[...].reshape(2 * block, width), x_ref[...], preferred_element_type=jnp.float32)
        value = value.reshape(2, block, cols)
        if before is not None:
            value = value + refs[4][...]
        own = value[1].astype(jnp.bfloat16)
        mean = (value[0] / n_ref[...].astype(jnp.float32)).astype(jnp.bfloat16)
        out = jnp.dot(own, w_ref[0], preferred_element_type=jnp.float32)
        out = out + jnp.dot(mean, w_ref[1], preferred_element_type=jnp.float32)
        o_ref[...] = out
        s_ref[...] = out.astype(jnp.bfloat16)

    specs = [
        pl.BlockSpec((2, block, width), lambda i: (0, i, 0)),
        pl.BlockSpec((width, cols), lambda i: (0, 0)),
        pl.BlockSpec((block, 1), lambda i: (i, 0)),
        pl.BlockSpec((2, cols, hidden), lambda i: (0, 0, 0)),
    ]
    operands = [counts, rows, count_a, weight]
    if before is not None:
        specs.append(pl.BlockSpec((2, block, cols), lambda i: (0, i, 0)))
        operands.append(before)
    out_spec = pl.BlockSpec((block, hidden), lambda i: (i, 0))
    return pl.pallas_call(
        body,
        grid=(hops // block,),
        in_specs=specs,
        out_specs=[out_spec, out_spec],
        out_shape=[
            jax.ShapeDtypeStruct((hops, hidden), jnp.float32),
            jax.ShapeDtypeStruct((hops, hidden), jnp.bfloat16),
        ],
        cost_estimate=pl.CostEstimate(flops=4 * hops * width * cols, bytes_accessed=10**7, transcendentals=0),
        name="first_layer",
    )(*operands)


def second_layer(own, other, bias_a, counts, count_b, weight, bias_b):
    hops, hidden = own.shape
    half = hidden // 2
    seeds = counts.shape[1]

    def body(own_ref, other_ref, ba_ref, c_ref, n_ref, w_ref, bb_ref, o_ref):
        other_value = other_ref[...].astype(jnp.float32)
        turned = jnp.concatenate([other_value[:, half:], other_value[:, :half]], axis=1)
        value = own_ref[...] + turned + ba_ref[...]
        value = jnp.maximum(value, 0.0).astype(jnp.bfloat16)
        picked = jnp.dot(c_ref[...].reshape(2 * seeds, hops), value, preferred_element_type=jnp.float32)
        self_b = picked[seeds:].astype(jnp.bfloat16)
        mean_b = (picked[:seeds] / n_ref[...].astype(jnp.float32)).astype(jnp.bfloat16)
        state = jnp.dot(self_b, w_ref[0], preferred_element_type=jnp.float32)
        state = state + jnp.dot(mean_b, w_ref[1], preferred_element_type=jnp.float32)
        state = jnp.maximum(state + bb_ref[...], 0.0)
        squares = jnp.sum(state * state, axis=1, keepdims=True)
        mine = state[:, :half] * jnp.sqrt(jnp.float32(hidden)) / jnp.sqrt(squares + hidden)
        o_ref[...] = mine.astype(jnp.bfloat16)

    return pl.pallas_call(
        body,
        out_shape=jax.ShapeDtypeStruct((seeds, half), jnp.bfloat16),
        cost_estimate=pl.CostEstimate(flops=10**9, bytes_accessed=10**7, transcendentals=0),
        name="second_layer",
    )(own, other, bias_a, counts, count_b, weight, bias_b)


def shards(
    n_dom,
    table,
    weight_a,
    bias_a,
    weight_b,
    bias_b,
    requests,
    near_a,
    self_a,
    count_a,
    near_b,
    self_b,
    count_b,
):
    features = table.shape[1]
    half = weight_a.shape[1]
    per = requests.shape[2]
    mine = lax.axis_index("mp")
    pair = 1 - mine
    swap = [(0, 1), (1, 0)]
    spans = spans_of(per)

    asked = lax.all_to_all(requests[0], "dom", split_axis=0, concat_axis=0, tiled=True)

    place_fn = functools.partial(place_of, per=per, owners=n_dom, spans=spans)
    widths = [n_dom * (high - low) for low, high in spans]
    tab_a = jnp.concatenate([near_a, self_a[:, None], count_a[:, None]], axis=1)
    counts = count_matrices(tab_a, near_a.shape[1], place_fn, widths)
    tab_b = jnp.concatenate([near_b, self_b[:, None], count_b[:, None]], axis=1)
    (counts_b,) = count_matrices(tab_b, near_b.shape[1], lambda value: value, [near_a.shape[0]])

    arrived = []
    for low, high in spans:
        found = table[asked[:, low:high]]
        moved = lax.all_to_all(found, "dom", split_axis=0, concat_axis=0, tiled=True)
        arrived.append(moved.reshape(-1, features))

    split_a = weight_a.reshape(2, 2, features, half)
    mine_a = lax.dynamic_index_in_dim(split_a, mine, 1, keepdims=False)
    send_a = lax.dynamic_index_in_dim(split_a, pair, 1, keepdims=False)
    whole_a = jnp.concatenate([mine_a, lax.ppermute(send_a, "mp", swap)], axis=2)

    def turned(value):
        value = value.reshape((-1, 2, half) + value.shape[1:])
        first = lax.dynamic_index_in_dim(value, mine, 1)
        second = lax.dynamic_index_in_dim(value, pair, 1)
        return jnp.concatenate([first, second], axis=1)

    all_b = jnp.concatenate([weight_b, lax.ppermute(weight_b, "mp", swap)], axis=1)
    whole_b = turned(all_b).reshape(2, 2 * half, 2 * half)
    whole_bias_a = turned(bias_a).reshape(1, 2 * half)
    whole_bias_b = turned(bias_b).reshape(1, 2 * half)

    tail = (whole_a, whole_b, whole_bias_a, whole_bias_b, counts_b, count_a[:, None], count_b[:, None])
    arrived, tail = lax.optimization_barrier((arrived, tail))
    whole_a, whole_b, whole_bias_a, whole_bias_b, counts_b, count_a, count_b = tail

    before = None
    for number in range(len(spans) - 1):
        before = gather_sums(counts[number], arrived[number], before)
    own, send = first_layer(counts[-1], arrived[-1], before, count_a, whole_a)
    other = lax.ppermute(send, "mp", swap)
    return second_layer(own, other, whole_bias_a, counts_b, count_b, whole_b, whole_bias_b)


def solution(mesh):
    placed = (
        P("dom", "mp"),
        P(None, "mp"),
        P(),
        P(None, "mp"),
        P(),
        P("dom", None, None),
        P("dom", None),
        P("dom"),
        P("dom"),
        P("dom", None),
        P("dom"),
        P("dom"),
    )
    return jax.shard_map(
        functools.partial(shards, mesh.shape["dom"]),
        mesh=mesh,
        in_specs=placed,
        out_specs=P("dom", "mp"),
        check_vma=False,
    )
```

time: 136 us -> 83.4 us (0.61)
  the two profiles are of different devices: /device:TPU:0 before, /device:TPU:13 now
where the time goes in v1:
time: 83.4 us; the launch traced here: 82.8 us
  Pallas kernels  31.5 us (38%)
  local copies, waits for them, and re-layouts  17.4 us (21%)
  blocking collectives  11 us (13%)
  starting transfers between devices  10.1 us (12%)
  other arithmetic  6.42 us (8%)
  waiting for transfers between devices  6.4 us (8%)
    pallas_call x2, Pallas kernels, count_matrices(): pl.pallas_call(body, out_shape=[jax.ShapeDtypeStruct((2, total, width), j...  17.4 us
    all_to_all x1, blocking collectives, shards(): lax.all_to_all(requests[0], 'dom', split_axis=0, concat_axis=0, tiled=True)  11 us
    pallas_call x1, Pallas kernels, first_layer(): pl.pallas_call(body, grid=(hops // block,), in_specs=specs, out_specs=[ou...  9.75 us
    gather x1, local copies, waits for them, and re-layouts, shards(): found = table[asked[:, low:high]]  9.04 us
    all_to_all x1, starting transfers between devices, shards(): lax.all_to_all(found, 'dom', split_axis=0, concat_axis=0, tiled=True)  6.23 us
    all_to_all x1, waiting for transfers between devices, shards(): lax.all_to_all(found, 'dom', split_axis=0, concat_axis=0, tiled=True)  4.55 us
    pallas_call x1, Pallas kernels, second_layer(): pl.pallas_call(body, out_shape=jax.ShapeDtypeStruct((seeds, half), jnp.bf...  4.35 us
    ppermute x1, starting transfers between devices, shards(): lax.ppermute(weight_b, 'mp', swap)  2.45 us
  transfers between devices with their start and end apart: 4, of which 2 were waited for; matrix products, arithmetic and copies ran while one was open for 17% of the time, Pallas kernels for 21%

profile of v1, /device:TPU:13, one launch (start us, length us, event | category | flops | bytes accessed | tf_op | source)
XLA Modules:
  0.0 82.8 jit_solution(12149955574393966084)
XLA Ops:
  0.0 11.0 %all_to_all.17 = s32[16,1,128]{2,1,0:T(1,128)S(1)} all-to-all(s32[16,1,128]{2,1,0:T(1,128)} %bitcast.38), channel_id=1, replica_groups=mesh['dom'=16,'mp'=2] {'dom'}, dimensions={0} | all-to-all | bytes 16384 | tf_op jit(solution)/shard_map/all_to_all | solution.py:213
  11.0 9.0 %gather_fusion = bf16[2048,384]{1,0:T(8,128)(2,1)} fusion(bf16[4096,384]{1,0:T(8,128)(2,1)S(1)} %copy-done, s32[2048]{0:T(1024)S(1)} %fusion.1), kind=kCustom, calls=%fused_computation | custom fusion | bytes 3153920 | tf_op jit(solution)/shard_map/gather | solution.py:224
  20.0 6.2 %all-to-all-start.1 = ((bf16[16,128,384]{2,1,0:T(8,128)(2,1)}), bf16[16,128,384]{2,1,0:T(8,128)(2,1)}, u32[]{:S(2)}, u32[]{:S(2)}) async-start(bf16[16,128,384]{2,1,0:T(8,128)(2,1)} %bitcast.29), calls=%async_computation.1 | async-start | bytes 3145728 | tf_op jit(solution)/shard_map/all_to_all | solution.py:225
  26.3 2.5 %collective-permute-start.1 = (bf16[1024,256]{1,0:T(8,128)(2,1)}, bf16[1024,256]{1,0:T(8,128)(2,1)}, u32[]{:S(2)}, u32[]{:S(2)}) collective-permute-start(bf16[1024,256]{1,0:T(8,128)(2,1)} %param.15), channel_id=1, source_target_pairs={{0,1},{1,0},{2,3},{3,2},{4,5},{5,4},{6,7},{7,6},{8,9},{9,8},{10,11... | collective-permute-start | bytes 1572872 | tf_op jit(solution)/shard_map/ppermute | solution.py:239
  28.7 1.9 %dynamic-slice_bitcast_fusion.1 = (bf16[2,384,256]{2,1,0:T(8,128)(2,1)S(1)}, bf16[2,384,256]{2,1,0:T(8,128)(2,1)}) fusion(bf16[2,2,384,256]{3,2,1,0:T(8,128)(2,1)} %bitcast.32, s32[]{:T(128)S(6)} %select_n.26, s32[]{:T(128)S(6)} %select_n.27), kind=kLoop, calls=%fused_computation.5 | loop fusion | bytes 1572872 | tf_op jit(solution)/shard_map/jit(dynamic_index_in_dim)/squeeze | solution.py:229
  30.7 0.7 reshape.61
  31.4 0.5 copy.35
  32.0 0.5 copy.36
  32.5 0.7 pad_add_fusion.1
  33.2 0.8 copy.30.tab_ref
  34.1 1.5 %pad_add_fusion = s32[1024,12]{0,1:T(8,128)} fusion(s32[1024,1]{0,1:T(1,128)S(1)} %bitcast.34, s32[1024,1]{0,1:T(1,128)} %bitcast.41, s32[1024,10]{0,1:T(8,128)} %param.18), kind=kLoop, calls=%fused_computation.6 | loop fusion | flops 24576 | bytes 98304 | tf_op jit(solution)/shard_map/concatenate | solution.py:217
  35.5 1.9 %copy.27.tab_ref = s32[1024,12]{1,0:T(8,128)} copy(s32[1024,12]{0,1:T(8,128)} %pad_add_fusion) | data formatting | bytes 98304 | tf_op jit(solution)/shard_map/concatenate | solution.py:217
  37.4 3.4 %shard_map.119.c_ref = bf16[2,256,1024]{2,1,0:T(8,128)(2,1)} custom-call(s32[256,7]{1,0:T(8,128)} %copy.30.tab_ref), custom_call_target="tpu_custom_call" | custom-call | flops 1000000000 | bytes 10000000 | tf_op jit(solution)/shard_map/pallas_call | solution.py:78
  40.8 14.0 %shard_map.118.refs_0_ = bf16[2,1024,2048]{2,1,0:T(8,128)(2,1)} custom-call(s32[1024,12]{1,0:T(8,128)} %copy.27.tab_ref), custom_call_target="tpu_custom_call" | custom-call | flops 1000000000 | bytes 10000000 | tf_op jit(solution)/shard_map/pallas_call | solution.py:78
  54.8 2.0 %pad_maximum_fusion.2.refs_3_ = bf16[2,384,512]{2,1,0:T(8,128)(2,1)} fusion(bf16[2,384,256]{2,1,0:T(8,128)(2,1)} %collective-permute-done, bf16[2,384,256]{2,1,0:T(8,128)(2,1)S(1)} %get-tuple-element.27), kind=kLoop, calls=%fused_computation.3 | loop fusion | flops 1572864 | bytes 1572864 | tf_op jit(solution)/shard_map/concatenate | solution.py:231
  56.8 1.1 %pad_maximum_fusion = bf16[1024,512]{1,0:T(8,128)(2,1)S(1)} fusion(bf16[1024,256]{1,0:T(8,128)(2,1)} %collective-permute-done.1, bf16[1024,256]{1,0:T(8,128)(2,1)S(1)} %copy-done.1), kind=kLoop, calls=%fused_computation.1 | loop fusion | flops 2097152 | bytes 2097152 | tf_op jit(solution)/shard_map/concatenate | solution.py:239
  58.0 1.1 %pad_maximum_fusion.1 = bf16[2,2,256,512]{3,2,1,0:T(8,128)(2,1)} fusion(bf16[2,1,256,512]{3,2,1,0:T(8,128)(2,1)S(1)} %get-tuple-element.26, bf16[2,1,256,512]{3,2,1,0:T(8,128)(2,1)S(1)} %get-tuple-element.25), kind=kLoop, calls=%fused_computation.2 | loop fusion | flops 524288 | bytes 2097152 | tf_op jit(solution)/shard_map/concatenate | solution.py:237
  59.1 4.6 %all-to-all-done.1 = bf16[16,128,384]{2,1,0:T(8,128)(2,1)} async-done(((bf16[16,128,384]{2,1,0:T(8,128)(2,1)}), bf16[16,128,384]{2,1,0:T(8,128)(2,1)}, u32[]{:S(2)}, u32[]{:S(2)}) %all-to-all-start.1) | async-done | bytes 1572896 | tf_op jit(solution)/shard_map/all_to_all | solution.py:225
  63.6 1.0 %copy.31.refs_2_ = s32[1024,1]{1,0:T(8,128)} copy(s32[1024,1]{0,1:T(1,128)S(1)} %bitcast.35) | data formatting | bytes 8192 | tf_op jit(solution)/shard_map/optimization_barrier | solution.py:245
  64.7 9.8 %first_layer.1 = (f32[1024,512]{1,0:T(8,128)}, bf16[1024,512]{1,0:T(8,128)(2,1)}) custom-call(bf16[2,1024,2048]{2,1,0:T(8,128)(2,1)} %shard_map.118.refs_0_, bf16[2048,384]{1,0:T(8,128)(2,1)} %bitcast.6.refs_1_, s32[1024,1]{1,0:T(8,128)} %copy.31.refs_2_, bf16[2,384,512]{2,1,0:T(8,128)(2,1)} %pad_maximum_fusion.2.refs_3_), custom_call_target="tpu_custom_call" | custom-call | flops 3221225472 | bytes 10000000 | tf_op jit(solution)/shard_map/first_layer/pallas_call | solution.py:148
  74.4 1.4 %collective-permute-start.2 = (bf16[1024,512]{1,0:T(8,128)(2,1)}, bf16[1024,512]{1,0:T(8,128)(2,1)}, u32[]{:S(2)}, u32[]{:S(2)}) collective-permute-start(bf16[1024,512]{1,0:T(8,128)(2,1)} %get-tuple-element.19), channel_id=1, source_target_pairs={{0,1},{1,0},{2,3},{3,2},{4,5},{5,4},{6,7},{7,6},{8,9},{9,8},{10,11... | collective-permute-start | bytes 3145736 | tf_op jit(solution)/shard_map/ppermute | solution.py:252
  75.9 0.8 copy.32.n_ref
  76.6 1.8 %collective-permute-done.2.other_ref = bf16[1024,512]{1,0:T(8,128)(2,1)} collective-permute-done((bf16[1024,512]{1,0:T(8,128)(2,1)}, bf16[1024,512]{1,0:T(8,128)(2,1)}, u32[]{:S(2)}, u32[]{:S(2)}) %collective-permute-start.2) | collective-permute-done | bytes 1048608 | tf_op jit(solution)/shard_map/ppermute | solution.py:252
  78.5 4.3 %second_layer.1 = bf16[256,256]{1,0:T(8,128)(2,1)} custom-call(f32[1024,512]{1,0:T(8,128)} %get-tuple-element.18.own_ref, bf16[1024,512]{1,0:T(8,128)(2,1)} %collective-permute-done.2.other_ref, f32[1,512]{1,0:T(1,128)} %bitcast.36, bf16[2,256,1024]{2,1,0:T(8,128)(2,1)} %shard_map.119.c_ref, s32[256,1]{1,0:T(8,128)} %copy.32.n_ref, ...), custom_call_target="tpu_custom_call" | custom-call | flops 1000000000 | bytes 10000000 | tf_op jit(solution)/shard_map/second_layer/pallas_call | solution.py:182
  (19 shorter events, 0.2 us)
Async XLA Ops:
  0.0 11.0 %copy-start = (bf16[4096,384]{1,0:T(8,128)(2,1)S(1)}, bf16[4096,384]{1,0:T(8,128)(2,1)}, u32[]{:S(2)}) copy-start(bf16[4096,384]{1,0:T(8,128)(2,1)} %param.12) | copy-start | bytes 9437188
  20.0 43.6 %all-to-all-start.1 = ((bf16[16,128,384]{2,1,0:T(8,128)(2,1)}), bf16[16,128,384]{2,1,0:T(8,128)(2,1)}, u32[]{:S(2)}, u32[]{:S(2)}) async-start(bf16[16,128,384]{2,1,0:T(8,128)(2,1)} %bitcast.29), calls=%async_computation.1 | async-start | bytes 3145728 | tf_op jit(solution)/shard_map/all_to_all | solution.py:225
  26.3 4.4 %copy-start.4 = (f32[512]{0:T(512)S(1)}, f32[512]{0:T(512)}, u32[]{:S(2)}) copy-start(f32[512]{0:T(512)} %param.14) | copy-start | bytes 6148
  26.3 6.3 %copy-start.3 = (s32[256]{0:T(256)S(1)}, s32[256]{0:T(256)}, u32[]{:S(2)}) copy-start(s32[256]{0:T(256)} %param.23) | copy-start | bytes 3076
  26.3 7.8 %copy-start.2 = (s32[1024]{0:T(1024)S(1)}, s32[1024]{0:T(1024)}, u32[]{:S(2)}) copy-start(s32[1024]{0:T(1024)} %param.20) | copy-start | bytes 12292
  26.3 30.5 %collective-permute-start.1 = (bf16[1024,256]{1,0:T(8,128)(2,1)}, bf16[1024,256]{1,0:T(8,128)(2,1)}, u32[]{:S(2)}, u32[]{:S(2)}) collective-permute-start(bf16[1024,256]{1,0:T(8,128)(2,1)} %param.15), channel_id=1, source_target_pairs={{0,1},{1,0},{2,3},{3,2},{4,5},{5,4},{6,7},{7,6},{8,9},{9,8},{10,11... | collective-permute-start | bytes 1572872 | tf_op jit(solution)/shard_map/ppermute | solution.py:239
  30.7 24.1 %collective-permute-start = (bf16[2,384,256]{2,1,0:T(8,128)(2,1)}, bf16[2,384,256]{2,1,0:T(8,128)(2,1)}, u32[]{:S(2)}, u32[]{:S(2)}) collective-permute-start(bf16[2,384,256]{2,1,0:T(8,128)(2,1)} %get-tuple-element.28), channel_id=1, source_target_pairs={{0,1},{1,0},{2,3},{3,2},{4,5},{5,4},{6,7},{7,6},{8,9},{9,8},{10,11... | collective-permute-start | bytes 1179656 | tf_op jit(solution)/shard_map/ppermute | solution.py:231
  54.8 2.0 %copy-start.1 = (bf16[1024,256]{1,0:T(8,128)(2,1)S(1)}, bf16[1024,256]{1,0:T(8,128)(2,1)}, u32[]{:S(2)}) copy-start(bf16[1024,256]{1,0:T(8,128)(2,1)} %param.15) | copy-start | bytes 1572868
  74.4 4.1 %collective-permute-start.2 = (bf16[1024,512]{1,0:T(8,128)(2,1)}, bf16[1024,512]{1,0:T(8,128)(2,1)}, u32[]{:S(2)}, u32[]{:S(2)}) collective-permute-start(bf16[1024,512]{1,0:T(8,128)(2,1)} %get-tuple-element.19), channel_id=1, source_target_pairs={{0,1},{1,0},{2,3},{3,2},{4,5},{5,4},{6,7},{7,6},{8,9},{9,8},{10,11... | collective-permute-start | bytes 3145736 | tf_op jit(solution)/shard_map/ppermute | solution.py:252

commit v2 on v0

v2 whole, which is shorter than its diff:
```python
import functools

import jax
import jax.numpy as jnp
from jax import lax
from jax.experimental import pallas as pl
from jax.experimental.pallas import tpu as pltpu
from jax.sharding import PartitionSpec as P


LANES = 128
PICK = 2048
BATCHES = ((8, 13), (0, 1, 4, 5, 9, 12))


def split_index(value, size):
    if size & (size - 1) == 0:
        return lax.shift_right_logical(value, size.bit_length() - 1), value & (size - 1)
    quotient = lax.div(value, size)
    return quotient, value - quotient * size


def estimate(flops):
    return pl.CostEstimate(flops=flops, bytes_accessed=10**7, transcendentals=0)


def count_matrices(near, own, count, me, place_fn, widths):
    fan, total = near.shape
    block = min(2 * LANES, total)
    bits = max(1, fan.bit_length())
    fields = 32 // bits
    tall = min(LANES // 2, min(widths))

    def body(me_ref, near_ref, own_ref, count_ref, *outs):
        pieces = [(ref, at) for ref in outs for at in range(ref.shape[1] // LANES)]
        words = -(-len(pieces) // fields)
        rank = lax.broadcasted_iota(jnp.int32, (fan, LANES), 0)
        for lane in range(block // LANES):
            cols = slice(lane * LANES, (lane + 1) * LANES)
            place = place_fn(near_ref[:, cols], me_ref)
            group, low = split_index(place, LANES)
            word, field = split_index(group, fields)
            unit = jnp.left_shift(jnp.ones_like(field), field * bits)
            unit = jnp.where((rank < count_ref[:, cols]) & (place >= 0), unit, 0)
            units = [jnp.where(word == w, unit, 0) for w in range(words)]
            mine = place_fn(own_ref[:, cols], me_ref)
            for top in range(0, LANES, tall):
                rows = lax.broadcasted_iota(jnp.int32, (tall, LANES), 0) + top
                sums = [jnp.zeros((tall, LANES), jnp.int32) for _ in range(words)]
                for j in range(fan):
                    hit = rows == low[j : j + 1, :]
                    for w in range(words):
                        sums[w] = sums[w] + jnp.where(hit, units[w][j : j + 1, :], 0)
                for number, (ref, part) in enumerate(pieces):
                    found = lax.shift_right_logical(sums[number // fields], bits * (number % fields))
                    found = (found & ((1 << bits) - 1)).astype(jnp.float32)
                    here = slice(part * LANES + top, part * LANES + top + tall)
                    ref[0, here, cols] = found.astype(jnp.bfloat16)
                    one = jnp.where(rows == mine - number * LANES, 1.0, 0.0)
                    ref[1, here, cols] = one.astype(jnp.bfloat16)

    line = pl.BlockSpec((1, block), lambda i: (0, i))
    return pl.pallas_call(
        body,
        grid=(total // block,),
        in_specs=[
            pl.BlockSpec(memory_space=pltpu.SMEM),
            pl.BlockSpec((fan, block), lambda i: (0, i)),
            line,
            line,
        ],
        out_specs=[pl.BlockSpec((2, width, block), lambda i: (0, 0, i)) for width in widths],
        out_shape=[jax.ShapeDtypeStruct((2, width, total), jnp.bfloat16) for width in widths],
        cost_estimate=estimate(10**9),
    )(me, near, own, count)


def pick_rows(asked, where, table, their_table, distances, step):
    nodes, share = table.shape
    per = asked.shape[1]
    block = min(PICK, nodes)
    total = len(distances) * per

    def body(at_ref, ask_ref, mine_ref, their_ref, *refs):
        outs, acc, ids = refs[:-2], refs[-2], refs[-1]
        now = pl.program_id(0)

        @pl.when(now == 0)
        def _():
            acc[...] = jnp.zeros_like(acc)
            for number, base in enumerate(distances):
                partner = at_ref[0] ^ (base ^ (step * at_ref[1]))
                line = ask_ref[pl.ds(partner, 1), :]
                ids[number * per : (number + 1) * per, :] = jnp.broadcast_to(line, (LANES, per)).T

        lanes = lax.broadcasted_iota(jnp.int32, (total, LANES), 1) + now * block
        wanted = ids[...]
        marks = [
            jnp.where(wanted - at == lanes, 1.0, 0.0).astype(jnp.bfloat16) for at in range(0, block, LANES)
        ]
        marks = jnp.concatenate(marks, axis=1)
        table_rows = jnp.concatenate([mine_ref[...], their_ref[...]], axis=1)
        acc[...] += jnp.dot(marks, table_rows, preferred_element_type=jnp.float32)

        @pl.when(now == pl.num_programs(0) - 1)
        def _():
            for number, ref in enumerate(outs):
                ref[...] = acc[number * per : (number + 1) * per, :].astype(jnp.bfloat16)

    rows = pl.BlockSpec((block, share), lambda i: (i, 0))
    return pl.pallas_call(
        body,
        grid=(nodes // block,),
        in_specs=[
            pl.BlockSpec(memory_space=pltpu.SMEM),
            pl.BlockSpec(asked.shape, lambda i: (0, 0)),
            rows,
            rows,
        ],
        out_specs=[pl.BlockSpec((per, 2 * share), lambda i: (0, 0))] * len(distances),
        out_shape=[jax.ShapeDtypeStruct((per, 2 * share), jnp.bfloat16)] * len(distances),
        scratch_shapes=[pltpu.VMEM((total, 2 * share), jnp.float32), pltpu.VMEM((total, LANES), jnp.int32)],
        cost_estimate=estimate(4 * total * nodes * share),
    )(where, asked, table, their_table)


def first_layer(counts, count, rows, core, weight, their_weight, before=None, last=False):
    _, width, total = counts.shape
    cols = rows[0].shape[1]
    features, half = weight.shape[0] // 2, weight.shape[1]
    share = cols if cols < features else features // 2
    block = min(2 * LANES, total)
    have = before is not None

    def body(core_ref, c_ref, n_ref, *refs):
        refs = list(refs)
        row_refs = [refs.pop(0) for _ in rows]
        shard_refs = (refs.pop(0), refs.pop(0))
        old_ref = refs.pop(0) if have else None
        o_ref, turned = refs

        @pl.when(pl.program_id(0) == 0)
        def _():
            core_value = core_ref[0]
            first = pl.multiple_of(core_value * share, LANES)
            second = pl.multiple_of((1 - core_value) * share, LANES)
            spots = (first, second) if cols > share else (first,)
            value = jnp.concatenate([ref[...] for ref in row_refs], axis=0)
            for number, ref in enumerate(shard_refs):
                hidden_at = core_value * half if number == 0 else (1 - core_value) * half
                here = pl.ds(pl.multiple_of(hidden_at, LANES), half)
                for part in range(2):
                    pieces = [ref[pl.ds(part * features + at, share), :] for at in spots]
                    piece = jnp.concatenate(pieces, axis=0)
                    product = jnp.dot(value, piece, preferred_element_type=jnp.float32)
                    turned[part, here, :] = product.astype(jnp.bfloat16).T

        out = jnp.dot(turned[1], c_ref[0], preferred_element_type=jnp.float32)
        out = out * (1.0 / n_ref[...].astype(jnp.float32))
        out = out + jnp.dot(turned[0], c_ref[1], preferred_element_type=jnp.float32)
        if have:
            out = out + old_ref[...]
        o_ref[...] = out.astype(o_ref.dtype)

    out_spec = pl.BlockSpec((2 * half, block), lambda i: (0, i))
    specs = [
        pl.BlockSpec(memory_space=pltpu.SMEM),
        pl.BlockSpec((2, width, block), lambda i: (0, 0, i)),
        pl.BlockSpec((1, block), lambda i: (0, i)),
    ]
    specs += [pl.BlockSpec(piece.shape, lambda i: (0, 0)) for piece in rows]
    specs += [pl.BlockSpec(weight.shape, lambda i: (0, 0))] * 2
    operands = [core, counts, count, *rows, weight, their_weight]
    if have:
        specs.append(out_spec)
        operands.append(before)
    return pl.pallas_call(
        body,
        grid=(total // block,),
        in_specs=specs,
        out_specs=out_spec,
        out_shape=jax.ShapeDtypeStruct((2 * half, total), jnp.bfloat16 if last else jnp.float32),
        scratch_shapes=[pltpu.VMEM((2, 2 * half, width), jnp.bfloat16)],
        cost_estimate=estimate(4 * width * total * cols),
    )(*operands)


def second_layer(own, other, bias_a, counts, count, core, weight, their_weight, bias_b):
    hidden, _ = own.shape
    half = hidden // 2
    seeds = counts.shape[2]

    def body(core_ref, own_ref, other_ref, ba_ref, c_ref, n_ref, w_ref, t_ref, bb_ref, o_ref):
        bias = jnp.broadcast_to(ba_ref[...], (LANES, hidden)).T[:, :1]
        value = own_ref[...].astype(jnp.float32) + other_ref[...].astype(jnp.float32) + bias
        value = jnp.maximum(value, 0.0).astype(jnp.bfloat16)
        self_b = jnp.dot(value, c_ref[1], preferred_element_type=jnp.float32)
        mean_b = jnp.dot(value, c_ref[0], preferred_element_type=jnp.float32)
        mean_b = mean_b * (1.0 / n_ref[...].astype(jnp.float32))
        self_b = self_b.T.astype(jnp.bfloat16)
        mean_b = mean_b.T.astype(jnp.bfloat16)

        def state_of(ref, index):
            state = jnp.dot(self_b, ref[:hidden, :], preferred_element_type=jnp.float32)
            state = state + jnp.dot(mean_b, ref[hidden:, :], preferred_element_type=jnp.float32)
            return jnp.maximum(state + bb_ref[pl.ds(index, 1), :], 0.0)

        state = state_of(w_ref, core_ref[0])
        theirs = state_of(t_ref, 1 - core_ref[0])
        squares = jnp.sum(state * state + theirs * theirs, axis=1, keepdims=True)
        scale = jnp.sqrt(jnp.float32(hidden)) / jnp.sqrt(squares + hidden)
        o_ref[...] = (state * scale).astype(jnp.bfloat16)

    whole = pl.BlockSpec(memory_space=pltpu.VMEM)
    return pl.pallas_call(
        body,
        in_specs=[pl.BlockSpec(memory_space=pltpu.SMEM)] + [whole] * 8,
        out_shape=jax.ShapeDtypeStruct((seeds, half), jnp.bfloat16),
        cost_estimate=estimate(10**9),
        name="second_layer",
    )(core, own, other, bias_a, counts, count, weight, their_weight, bias_b)


def plan_of(n_dom):
    if n_dom != 16:
        return None
    return n_dom // 8, (8, 13, 0, 1), (4, 5, 9, 12)


def shards(
    n_dom,
    table,
    weight_a,
    bias_a,
    weight_b,
    bias_b,
    requests,
    near_a,
    self_a,
    count_a,
    near_b,
    self_b,
    count_b,
):
    features = table.shape[1]
    half = weight_a.shape[1]
    per = requests.shape[2]
    me = lax.axis_index("dom")
    core = lax.axis_index("mp")
    core_line = core.reshape(1).astype(jnp.int32)
    where = jnp.stack([me, core]).astype(jnp.int32)
    swap = [(0, 1), (1, 0)]
    plan = plan_of(n_dom)

    def place_fn(slots, at_ref):
        if plan is None:
            return slots
        step, early, late = plan
        owner, row = split_index(slots, per)
        distance = owner ^ at_ref[0]
        rank = jnp.full_like(slots, -2 * n_dom)
        for number, base in enumerate(early + late):
            rank = jnp.where(distance == base ^ (step * at_ref[1]), number, rank)
        return rank * per + row

    if plan is not None:
        their_table = lax.ppermute(table, "mp", swap)
    asked = lax.all_to_all(requests[0], "dom", split_axis=0, concat_axis=0, tiled=True)

    widths = [n_dom * per] if plan is None else [len(part) * per for part in plan[1:]]
    if plan is not None:
        near_a, their_table = lax.optimization_barrier((near_a, their_table))
    counts = count_matrices(near_a.T, self_a[None], count_a[None], where, place_fn, widths)
    (counts_b,) = count_matrices(
        near_b.T, self_b[None], count_b[None], where, lambda value, _: value, [near_a.shape[0]]
    )

    if plan is None:
        found = table.at[asked].get(mode="promise_in_bounds")
        moved = lax.all_to_all(found, "dom", split_axis=0, concat_axis=0, tiled=True)
        early, late = [], [moved.reshape(-1, features)]
    else:
        step = plan[0]
        found = {}
        for bases in BATCHES:
            picked = pick_rows(asked, where, table, their_table, bases, step)
            found.update(zip(bases, picked))

        def trade(base):
            pairs = [
                (2 * i + c, 2 * (i ^ (base ^ (step * c))) + c) for i in range(n_dom) for c in range(2)
            ]
            return lax.ppermute(found[base], ("dom", "mp"), pairs)

        early = [trade(base) for base in plan[1]]
        late = [trade(base) for base in plan[2]]

    their_a = lax.ppermute(weight_a, "mp", swap)
    their_b = lax.ppermute(weight_b, "mp", swap)
    count_line = count_a[None]
    before = None
    if early:
        early, (their_a, their_b, counts_b) = lax.optimization_barrier((early, (their_a, their_b, counts_b)))
        before = first_layer(counts[0], count_line, early, core_line, weight_a, their_a)
    own = first_layer(counts[-1], count_line, late, core_line, weight_a, their_a, before, last=True)
    other = lax.ppermute(own, "mp", swap)
    return second_layer(
        own, other, bias_a[None], counts_b, count_b[None], core_line, weight_b, their_b, bias_b.reshape(2, half)
    )


def solution(mesh):
    placed = (
        P("dom", "mp"),
        P(None, "mp"),
        P(),
        P(None, "mp"),
        P(),
        P("dom", None, None),
        P("dom", None),
        P("dom"),
        P("dom"),
        P("dom", None),
        P("dom"),
        P("dom"),
    )
    n_dom = mesh.shape["dom"]
    return jax.shard_map(
        functools.partial(shards, n_dom),
        mesh=mesh,
        in_specs=placed,
        out_specs=P("dom", "mp"),
        check_vma=False,
    )
```

time: 136 us -> 75.9 us (0.56)
  the two profiles are of different devices: /device:TPU:0 before, /device:TPU:9 now
where the time goes in v2:
time: 75.9 us; the launch traced here: 75.4 us
  Pallas kernels  37.4 us (49%)
  starting transfers between devices  22.5 us (30%)
  waiting for transfers between devices  11.2 us (15%)
  local copies, waits for them, and re-layouts  3.54 us (5%)
    ppermute x8, starting transfers between devices, trade(): return lax.ppermute(found[base], ('dom', 'mp'), pairs)  14 us
    pallas_call x2, Pallas kernels, pick_rows(): pl.pallas_call(body, grid=(nodes // block,), in_specs=[pl.BlockSpec(memor...  13.3 us
    pallas_call x2, Pallas kernels, first_layer(): pl.pallas_call(body, grid=(total // block,), in_specs=specs, out_specs=ou...  13.2 us
    all_to_all x1, starting transfers between devices, shards(): lax.all_to_all(requests[0], 'dom', split_axis=0, concat_axis=0, tiled=True)  6.66 us
    pallas_call x2, Pallas kernels, count_matrices(): pl.pallas_call(body, grid=(total // block,), in_specs=[pl.BlockSpec(memor...  6.57 us
    ppermute x8, waiting for transfers between devices, trade(): return lax.ppermute(found[base], ('dom', 'mp'), pairs)  5.55 us
    pallas_call x1, Pallas kernels, second_layer(): pl.pallas_call(body, in_specs=[pl.BlockSpec(memory_space=pltpu.SMEM)] + [...  4.32 us
    all_to_all x1, waiting for transfers between devices, shards(): lax.all_to_all(requests[0], 'dom', split_axis=0, concat_axis=0, tiled=True)  3.77 us
  transfers between devices with their start and end apart: 13, of which 4 were waited for; matrix products, arithmetic and copies ran while one was open for 2% of the time, Pallas kernels for 35%

profile of v2, /device:TPU:9, one launch (start us, length us, event | category | flops | bytes accessed | tf_op | source)
XLA Modules:
  0.0 75.4 jit_solution(1854830320563705567)
XLA Ops:
  0.0 0.7 collective-permute-start
  0.7 6.7 %all-to-all-start = ((s32[16,1,128]{2,1,0:T(1,128)}), s32[16,1,128]{2,1,0:T(1,128)S(1)}, u32[]{:S(2)}, u32[]{:S(2)}) async-start(s32[16,1,128]{2,1,0:T(1,128)} %bitcast.16), calls=%async_computation | async-start | bytes 16384 | tf_op jit(solution)/shard_map/all_to_all | solution.py:268
  8.0 0.6 pad_add_fusion.me_ref.at_ref
  8.6 3.8 %all-to-all-done = s32[16,1,128]{2,1,0:T(1,128)S(1)} async-done(((s32[16,1,128]{2,1,0:T(1,128)}), s32[16,1,128]{2,1,0:T(1,128)S(1)}, u32[]{:S(2)}, u32[]{:S(2)}) %all-to-all-start) | async-done | bytes 8224 | tf_op jit(solution)/shard_map/all_to_all | solution.py:268
  12.3 0.6 copy-done.11
  12.9 4.8 %shard_map.120 = (bf16[128,768]{1,0:T(8,128)(2,1)}, bf16[128,768]{1,0:T(8,128)(2,1)}) custom-call(s32[2]{0:T(128)} %pad_add_fusion.me_ref.at_ref, s32[16,128]{1,0:T(8,128)} %bitcast.11, bf16[4096,384]{1,0:T(8,128)(2,1)} %mine_ref.3, bf16[4096,384]{1,0:T(8,128)(2,1)} %collective-permute-done.their_ref), custom_call_target="tpu_custom_call" | custom-call | flops 1610612736 | bytes 10000000 | tf_op jit(solution)/shard_map/pallas_call | solution.py:111
  18.1 3.0 %collective-permute-start.6 = (bf16[128,768]{1,0:T(8,128)(2,1)}, bf16[128,768]{1,0:T(8,128)(2,1)S(1)}, u32[]{:S(2)}, u32[]{:S(2)}) collective-permute-start(bf16[128,768]{1,0:T(8,128)(2,1)} %get-tuple-element.32), channel_id=1, source_target_pairs={{0,26},{1,31},{2,24},{3,29},{4,30},{5,27},{6,28},{7,25},{8,18},{9,... | collective-permute-start | bytes 589832 | tf_op jit(solution)/shard_map/ppermute | solution.py:293
  21.0 8.5 %shard_map.119 = (bf16[128,768]{1,0:T(8,128)(2,1)}, bf16[128,768]{1,0:T(8,128)(2,1)}, bf16[128,768]{1,0:T(8,128)(2,1)}, bf16[128,768]{1,0:T(8,128)(2,1)}, bf16[1...) custom-call(s32[2]{0:T(128)} %pad_add_fusion.me_ref.at_ref, s32[16,128]{1,0:T(8,128)} %bitcast.12, ...), custom_call_target="tpu_custom_call" | custom-call | flops 4831838208 | bytes 10000000 | tf_op jit(solution)/shard_map/pallas_call | solution.py:111
  29.5 2.3 %collective-permute-start.7 = (bf16[128,768]{1,0:T(8,128)(2,1)}, bf16[128,768]{1,0:T(8,128)(2,1)S(1)}, u32[]{:S(2)}, u32[]{:S(2)}) collective-permute-start(bf16[128,768]{1,0:T(8,128)(2,1)} %get-tuple-element.33), channel_id=1, source_target_pairs={{0,0},{1,5},{2,2},{3,7},{4,4},{5,1},{6,6},{7,3},{8,8},{9,13},{10,1... | collective-permute-start | bytes 589832 | tf_op jit(solution)/shard_map/ppermute | solution.py:293
  31.9 2.1 %collective-permute-start.8 = (bf16[128,768]{1,0:T(8,128)(2,1)}, bf16[128,768]{1,0:T(8,128)(2,1)S(1)}, u32[]{:S(2)}, u32[]{:S(2)}) collective-permute-start(bf16[128,768]{1,0:T(8,128)(2,1)} %get-tuple-element.34), channel_id=1, source_target_pairs={{0,2},{1,7},{2,0},{3,5},{4,6},{5,3},{6,4},{7,1},{8,10},{9,15},{10,... | collective-permute-start | bytes 589832 | tf_op jit(solution)/shard_map/ppermute | solution.py:293
  34.0 2.1 %shard_map.121.c_ref = bf16[2,1024,256]{2,1,0:T(8,128)(2,1)} custom-call(s32[2]{0:T(128)} %pad_add_fusion.me_ref.at_ref, s32[5,256]{1,0:T(8,128)} %bitcast.21, s32[1,256]{1,0:T(1,128)} %bitcast.23, s32[1,256]{1,0:T(1,128)} %bitcast.18), custom_call_target="tpu_custom_call" | custom-call | flops 1000000000 | bytes 10000000 | tf_op jit(solution)/shard_map/pallas_call | solution.py:63
  36.1 1.2 %collective-permute-start.1 = (bf16[128,768]{1,0:T(8,128)(2,1)}, bf16[128,768]{1,0:T(8,128)(2,1)S(1)}, u32[]{:S(2)}, u32[]{:S(2)}) collective-permute-start(bf16[128,768]{1,0:T(8,128)(2,1)} %get-tuple-element.27), channel_id=1, source_target_pairs={{0,8},{1,13},{2,10},{3,15},{4,12},{5,9},{6,14},{7,11},{8,0},{9,5},... | collective-permute-start | bytes 589832 | tf_op jit(solution)/shard_map/ppermute | solution.py:293
  37.3 1.3 %collective-permute-start.2 = (bf16[128,768]{1,0:T(8,128)(2,1)S(1)}, bf16[128,768]{1,0:T(8,128)(2,1)S(1)}, u32[]{:S(2)}, u32[]{:S(2)}) collective-permute-start(bf16[128,768]{1,0:T(8,128)(2,1)S(1)} %copy-done.15), channel_id=1, source_target_pairs={{0,10},{1,15},{2,8},{3,13},{4,14},{5,11},{6,12},{7,9},{8,2},{9,7},... | collective-permute-start | bytes 589832 | tf_op jit(solution)/shard_map/ppermute | solution.py:293
  39.0 1.7 %collective-permute-start.3 = (bf16[128,768]{1,0:T(8,128)(2,1)S(1)}, bf16[128,768]{1,0:T(8,128)(2,1)S(1)}, u32[]{:S(2)}, u32[]{:S(2)}) collective-permute-start(bf16[128,768]{1,0:T(8,128)(2,1)S(1)} %copy-done.14), channel_id=1, source_target_pairs={{0,18},{1,23},{2,16},{3,21},{4,22},{5,19},{6,20},{7,17},{8,26},{9,... | collective-permute-start | bytes 589832 | tf_op jit(solution)/shard_map/ppermute | solution.py:293
  40.7 2.1 %collective-permute-start.4 = (bf16[128,768]{1,0:T(8,128)(2,1)S(1)}, bf16[128,768]{1,0:T(8,128)(2,1)S(1)}, u32[]{:S(2)}, u32[]{:S(2)}) collective-permute-start(bf16[128,768]{1,0:T(8,128)(2,1)S(1)} %copy-done.13), channel_id=1, source_target_pairs={{0,24},{1,29},{2,26},{3,31},{4,28},{5,25},{6,30},{7,27},{8,16},{9,... | collective-permute-start | bytes 589832 | tf_op jit(solution)/shard_map/ppermute | solution.py:293
  42.8 4.5 %shard_map.118 = (bf16[2,512,1024]{2,1,0:T(8,128)(2,1)}, bf16[2,512,1024]{2,1,0:T(8,128)(2,1)}) custom-call(s32[2]{0:T(128)} %pad_add_fusion.me_ref.at_ref, s32[10,1024]{1,0:T(8,128)} %bitcast.20, s32[1,1024]{1,0:T(1,128)} %bitcast.22, s32[1,1024]{1,0:T(1,128)} %bitcast.13), custom_call_target="tpu_custom_call" | custom-call | flops 1000000000 | bytes 10000000 | tf_op jit(solution)/shard_map/pallas_call | solution.py:63
  47.4 0.6 copy-done.6
  48.0 6.5 %shard_map.122.refs_6_ = f32[512,1024]{1,0:T(8,128)} custom-call(s32[1]{0:T(128)} %bitcast.core_ref, bf16[2,512,1024]{2,1,0:T(8,128)(2,1)} %get-tuple-element.36.c_ref, s32[1,1024]{1,0:T(1,128)} %bitcast.14, bf16[128,768]{1,0:T(8,128)(2,1)} %copy-done.3, bf16[128,768]{1,0:T(8,128)(2,1)} %copy-done.4, bf16[128,768]{1,0:T(8,128)(2,1)} %copy-done.5, ...), custom_call_target="tpu_custom_call" | custom-call | flops 1610612736 | bytes 10000000 | tf_op jit(solution)/shard_map/pallas_call | solution.py:177
  54.5 5.1 %collective-permute-done.4.refs_3_ = bf16[128,768]{1,0:T(8,128)(2,1)S(1)} collective-permute-done((bf16[128,768]{1,0:T(8,128)(2,1)S(1)}, bf16[128,768]{1,0:T(8,128)(2,1)S(1)}, u32[]{:S(2)}, u32[]{:S(2)}) %collective-permute-start.4) | collective-permute-done | bytes 196640 | tf_op jit(solution)/shard_map/ppermute | solution.py:293
  59.6 0.7 copy-done.10
  60.3 6.7 %shard_map.123.own_ref = bf16[512,1024]{1,0:T(8,128)(2,1)} custom-call(s32[1]{0:T(128)} %bitcast.core_ref, bf16[2,512,1024]{2,1,0:T(8,128)(2,1)} %get-tuple-element.25.c_ref, s32[1,1024]{1,0:T(1,128)} %bitcast.15, bf16[128,768]{1,0:T(8,128)(2,1)} %copy-done.7, bf16[128,768]{1,0:T(8,128)(2,1)} %copy-done.8, bf16[128,768]{1,0:T(8,128)(2,1)} %copy-done.9, ...), custom_call_target="tpu_custom_call" | custom-call | flops 1610612736 | bytes 10000000 | tf_op jit(solution)/shard_map/pallas_call | solution.py:177
  68.2 1.9 %collective-permute-done.11.other_ref = bf16[512,1024]{1,0:T(8,128)(2,1)S(1)} collective-permute-done((bf16[512,1024]{1,0:T(8,128)(2,1)}, bf16[512,1024]{1,0:T(8,128)(2,1)S(1)}, u32[]{:S(2)}, u32[]{:S(2)}) %collective-permute-start.11) | collective-permute-done | bytes 1048608 | tf_op jit(solution)/shard_map/ppermute | solution.py:306
  70.1 1.0 %copy-done.1 = bf16[512,1024]{1,0:T(8,128)(2,1)} copy-done((bf16[512,1024]{1,0:T(8,128)(2,1)}, bf16[512,1024]{1,0:T(8,128)(2,1)S(1)}, u32[]{:S(2)}) %copy-start.1) | copy-done | bytes 1048600
  71.1 4.3 %second_layer.1 = bf16[256,256]{1,0:T(8,128)(2,1)} custom-call(s32[1]{0:T(128)} %bitcast.core_ref, bf16[512,1024]{1,0:T(8,128)(2,1)} %shard_map.123.own_ref, bf16[512,1024]{1,0:T(8,128)(2,1)} %copy-done.1, f32[1,512]{1,0:T(1,128)} %bitcast.17, bf16[2,1024,256]{2,1,0:T(8,128)(2,1)} %shard_map.121.c_ref, s32[1,256]{1,0:T(1,128)} %bitcast.19, ...), custom_call_target="tpu_custom_call" | custom-call | flops 1000000000 | bytes 10000000 | tf_op jit(solution)/shard_map/second_layer/pallas_call | solution.py:215
  (43 shorter events, 2.6 us)
Async XLA Ops:
  0.0 8.6 %collective-permute-start = (bf16[4096,384]{1,0:T(8,128)(2,1)}, bf16[4096,384]{1,0:T(8,128)(2,1)}, u32[]{:S(2)}, u32[]{:S(2)}) collective-permute-start(bf16[4096,384]{1,0:T(8,128)(2,1)} %mine_ref.3), channel_id=1, source_target_pairs={{0,1},{1,0},{2,3},{3,2},{4,5},{5,4},{6,7},{7,6},{8,9},{9,8},{10,11... | collective-permute-start | bytes 9437192 | tf_op jit(solution)/shard_map/ppermute | solution.py:267
  0.7 11.7 %all-to-all-start = ((s32[16,1,128]{2,1,0:T(1,128)}), s32[16,1,128]{2,1,0:T(1,128)S(1)}, u32[]{:S(2)}, u32[]{:S(2)}) async-start(s32[16,1,128]{2,1,0:T(1,128)} %bitcast.16), calls=%async_computation | async-start | bytes 16384 | tf_op jit(solution)/shard_map/all_to_all | solution.py:268
  7.3 28.7 %collective-permute-start.9 = (bf16[1536,256]{1,0:T(8,128)(2,1)}, bf16[1536,256]{1,0:T(8,128)(2,1)S(1)}, u32[]{:S(2)}, u32[]{:S(2)}) collective-permute-start(bf16[1536,256]{1,0:T(8,128)(2,1)} %refs_4_.3), channel_id=1, source_target_pairs={{0,1},{1,0},{2,3},{3,2},{4,5},{5,4},{6,7},{7,6},{8,9},{9,8},{10,11... | collective-permute-start | bytes 2359304 | tf_op jit(solution)/shard_map/ppermute | solution.py:298
  7.9 23.9 %collective-permute-start.10 = (bf16[1024,256]{1,0:T(8,128)(2,1)}, bf16[1024,256]{1,0:T(8,128)(2,1)S(1)}, u32[]{:S(2)}, u32[]{:S(2)}) collective-permute-start(bf16[1024,256]{1,0:T(8,128)(2,1)} %w_ref.1), channel_id=1, source_target_pairs={{0,1},{1,0},{2,3},{3,2},{4,5},{5,4},{6,7},{7,6},{8,9},{9,8},{10,11... | collective-permute-start | bytes 1572872 | tf_op jit(solution)/shard_map/ppermute | solution.py:299
  17.7 19.6 %collective-permute-start.5 = (bf16[128,768]{1,0:T(8,128)(2,1)}, bf16[128,768]{1,0:T(8,128)(2,1)S(1)}, u32[]{:S(2)}, u32[]{:S(2)}) collective-permute-start(bf16[128,768]{1,0:T(8,128)(2,1)} %get-tuple-element.31), channel_id=1, source_target_pairs={{0,16},{1,21},{2,18},{3,23},{4,20},{5,17},{6,22},{7,19},{8,24},{9,... | collective-permute-start | bytes 589832 | tf_op jit(solution)/shard_map/ppermute | solution.py:293
  18.1 21.0 %collective-permute-start.6 = (bf16[128,768]{1,0:T(8,128)(2,1)}, bf16[128,768]{1,0:T(8,128)(2,1)S(1)}, u32[]{:S(2)}, u32[]{:S(2)}) collective-permute-start(bf16[128,768]{1,0:T(8,128)(2,1)} %get-tuple-element.32), channel_id=1, source_target_pairs={{0,26},{1,31},{2,24},{3,29},{4,30},{5,27},{6,28},{7,25},{8,18},{9,... | collective-permute-start | bytes 589832 | tf_op jit(solution)/shard_map/ppermute | solution.py:293
  29.5 7.8 %copy-start.15 = (bf16[128,768]{1,0:T(8,128)(2,1)S(1)}, bf16[128,768]{1,0:T(8,128)(2,1)}, u32[]{:S(2)}) copy-start(bf16[128,768]{1,0:T(8,128)(2,1)} %get-tuple-element.28) | copy-start | bytes 589828
  29.5 9.5 %copy-start.14 = (bf16[128,768]{1,0:T(8,128)(2,1)S(1)}, bf16[128,768]{1,0:T(8,128)(2,1)}, u32[]{:S(2)}) copy-start(bf16[128,768]{1,0:T(8,128)(2,1)} %get-tuple-element.29) | copy-start | bytes 589828
  29.5 11.2 %copy-start.13 = (bf16[128,768]{1,0:T(8,128)(2,1)S(1)}, bf16[128,768]{1,0:T(8,128)(2,1)}, u32[]{:S(2)}) copy-start(bf16[128,768]{1,0:T(8,128)(2,1)} %get-tuple-element.30) | copy-start | bytes 589828
  29.5 11.2 %collective-permute-start.7 = (bf16[128,768]{1,0:T(8,128)(2,1)}, bf16[128,768]{1,0:T(8,128)(2,1)S(1)}, u32[]{:S(2)}, u32[]{:S(2)}) collective-permute-start(bf16[128,768]{1,0:T(8,128)(2,1)} %get-tuple-element.33), channel_id=1, source_target_pairs={{0,0},{1,5},{2,2},{3,7},{4,4},{5,1},{6,6},{7,3},{8,8},{9,13},{10,1... | collective-permute-start | bytes 589832 | tf_op jit(solution)/shard_map/ppermute | solution.py:293
  31.9 15.5 %copy-start.2 = (bf16[1024,256]{1,0:T(8,128)(2,1)}, bf16[1024,256]{1,0:T(8,128)(2,1)S(1)}, u32[]{:S(2)}) copy-start(bf16[1024,256]{1,0:T(8,128)(2,1)S(1)} %collective-permute-done.10.t_ref) | copy-start | bytes 1572868
  31.9 15.5 %collective-permute-start.8 = (bf16[128,768]{1,0:T(8,128)(2,1)}, bf16[128,768]{1,0:T(8,128)(2,1)S(1)}, u32[]{:S(2)}, u32[]{:S(2)}) collective-permute-start(bf16[128,768]{1,0:T(8,128)(2,1)} %get-tuple-element.34), channel_id=1, source_target_pairs={{0,2},{1,7},{2,0},{3,5},{4,6},{5,3},{6,4},{7,1},{8,10},{9,15},{10,... | collective-permute-start | bytes 589832 | tf_op jit(solution)/shard_map/ppermute | solution.py:293
  36.1 11.3 %copy-start = (bf16[1536,256]{1,0:T(8,128)(2,1)}, bf16[1536,256]{1,0:T(8,128)(2,1)S(1)}, u32[]{:S(2)}) copy-start(bf16[1536,256]{1,0:T(8,128)(2,1)S(1)} %collective-permute-done.9.refs_5_) | copy-start | bytes 2359300
  36.1 18.4 %collective-permute-start.1 = (bf16[128,768]{1,0:T(8,128)(2,1)}, bf16[128,768]{1,0:T(8,128)(2,1)S(1)}, u32[]{:S(2)}, u32[]{:S(2)}) collective-permute-start(bf16[128,768]{1,0:T(8,128)(2,1)} %get-tuple-element.27), channel_id=1, source_target_pairs={{0,8},{1,13},{2,10},{3,15},{4,12},{5,9},{6,14},{7,11},{8,0},{9,5},... | collective-permute-start | bytes 589832 | tf_op jit(solution)/shard_map/ppermute | solution.py:293
  37.3 10.1 %copy-start.3 = (bf16[128,768]{1,0:T(8,128)(2,1)}, bf16[128,768]{1,0:T(8,128)(2,1)S(1)}, u32[]{:S(2)}) copy-start(bf16[128,768]{1,0:T(8,128)(2,1)S(1)} %collective-permute-done.5.refs_0_) | copy-start | bytes 589828
  37.3 17.2 %collective-permute-start.2 = (bf16[128,768]{1,0:T(8,128)(2,1)S(1)}, bf16[128,768]{1,0:T(8,128)(2,1)S(1)}, u32[]{:S(2)}, u32[]{:S(2)}) collective-permute-start(bf16[128,768]{1,0:T(8,128)(2,1)S(1)} %copy-done.15), channel_id=1, source_target_pairs={{0,10},{1,15},{2,8},{3,13},{4,14},{5,11},{6,12},{7,9},{8,2},{9,7},... | collective-permute-start | bytes 589832 | tf_op jit(solution)/shard_map/ppermute | solution.py:293
  39.0 8.4 %copy-start.4 = (bf16[128,768]{1,0:T(8,128)(2,1)}, bf16[128,768]{1,0:T(8,128)(2,1)S(1)}, u32[]{:S(2)}) copy-start(bf16[128,768]{1,0:T(8,128)(2,1)S(1)} %collective-permute-done.6.refs_1_) | copy-start | bytes 589828
  39.0 15.5 %collective-permute-start.3 = (bf16[128,768]{1,0:T(8,128)(2,1)S(1)}, bf16[128,768]{1,0:T(8,128)(2,1)S(1)}, u32[]{:S(2)}, u32[]{:S(2)}) collective-permute-start(bf16[128,768]{1,0:T(8,128)(2,1)S(1)} %copy-done.14), channel_id=1, source_target_pairs={{0,18},{1,23},{2,16},{3,21},{4,22},{5,19},{6,20},{7,17},{8,26},{9,... | collective-permute-start | bytes 589832 | tf_op jit(solution)/shard_map/ppermute | solution.py:293
  40.7 6.7 %copy-start.5 = (bf16[128,768]{1,0:T(8,128)(2,1)}, bf16[128,768]{1,0:T(8,128)(2,1)S(1)}, u32[]{:S(2)}) copy-start(bf16[128,768]{1,0:T(8,128)(2,1)S(1)} %collective-permute-done.7.refs_2_) | copy-start | bytes 589828
  40.7 18.9 %collective-permute-start.4 = (bf16[128,768]{1,0:T(8,128)(2,1)S(1)}, bf16[128,768]{1,0:T(8,128)(2,1)S(1)}, u32[]{:S(2)}, u32[]{:S(2)}) collective-permute-start(bf16[128,768]{1,0:T(8,128)(2,1)S(1)} %copy-done.13), channel_id=1, source_target_pairs={{0,24},{1,29},{2,26},{3,31},{4,28},{5,25},{6,30},{7,27},{8,16},{9,... | collective-permute-start | bytes 589832 | tf_op jit(solution)/shard_map/ppermute | solution.py:293
  54.5 5.1 %copy-start.7 = (bf16[128,768]{1,0:T(8,128)(2,1)}, bf16[128,768]{1,0:T(8,128)(2,1)S(1)}, u32[]{:S(2)}) copy-start(bf16[128,768]{1,0:T(8,128)(2,1)S(1)} %collective-permute-done.1.refs_0_) | copy-start | bytes 589828
  54.5 5.1 %copy-start.8 = (bf16[128,768]{1,0:T(8,128)(2,1)}, bf16[128,768]{1,0:T(8,128)(2,1)S(1)}, u32[]{:S(2)}) copy-start(bf16[128,768]{1,0:T(8,128)(2,1)S(1)} %collective-permute-done.2.refs_1_) | copy-start | bytes 589828
  60.3 7.3 %copy-start.12 = (f32[512]{0:T(512)S(1)}, f32[512]{0:T(512)}, u32[]{:S(2)}) copy-start(f32[512]{0:T(512)} %param.16) | copy-start | bytes 6148
  67.0 3.1 %collective-permute-start.11 = (bf16[512,1024]{1,0:T(8,128)(2,1)}, bf16[512,1024]{1,0:T(8,128)(2,1)S(1)}, u32[]{:S(2)}, u32[]{:S(2)}) collective-permute-start(bf16[512,1024]{1,0:T(8,128)(2,1)} %shard_map.123.own_ref), channel_id=1, source_target_pairs={{0,1},{1,0},{2,3},{3,2},{4,5},{5,4},{6,7},{7,6},{8,9},{9,8},{10,11... | collective-permute-start | bytes 3145736 | tf_op jit(solution)/shard_map/ppermute | solution.py:306
  (5 other events, 8.1 us)

commit v3 on v2

--- a/solution.py
+++ b/solution.py
@@ -71,6 +71,7 @@
         ],
         out_specs=[pl.BlockSpec((2, width, block), lambda i: (0, 0, i)) for width in widths],
         out_shape=[jax.ShapeDtypeStruct((2, width, total), jnp.bfloat16) for width in widths],
+        compiler_params=pltpu.CompilerParams(vmem_limit_bytes=None),
         cost_estimate=estimate(10**9),
     )(me, near, own, count)
 
@@ -120,6 +121,7 @@
         out_specs=[pl.BlockSpec((per, 2 * share), lambda i: (0, 0))] * len(distances),
         out_shape=[jax.ShapeDtypeStruct((per, 2 * share), jnp.bfloat16)] * len(distances),
         scratch_shapes=[pltpu.VMEM((total, 2 * share), jnp.float32), pltpu.VMEM((total, LANES), jnp.int32)],
+        compiler_params=pltpu.CompilerParams(vmem_limit_bytes=32 * 2**20),
         cost_estimate=estimate(4 * total * nodes * share),
     )(where, asked, table, their_table)
 
@@ -129,7 +131,7 @@
     cols = rows[0].shape[1]
     features, half = weight.shape[0] // 2, weight.shape[1]
     share = cols if cols < features else features // 2
-    block = min(2 * LANES, total)
+    block = min(4 * LANES, total)
     have = before is not None
 
     def body(core_ref, c_ref, n_ref, *refs):
@@ -181,6 +183,7 @@
         out_specs=out_spec,
         out_shape=jax.ShapeDtypeStruct((2 * half, total), jnp.bfloat16 if last else jnp.float32),
         scratch_shapes=[pltpu.VMEM((2, 2 * half, width), jnp.bfloat16)],
+        compiler_params=pltpu.CompilerParams(vmem_limit_bytes=32 * 2**20),
         cost_estimate=estimate(4 * width * total * cols),
     )(*operands)
 
@@ -216,6 +219,7 @@
         body,
         in_specs=[pl.BlockSpec(memory_space=pltpu.SMEM)] + [whole] * 8,
         out_shape=jax.ShapeDtypeStruct((seeds, half), jnp.bfloat16),
+        compiler_params=pltpu.CompilerParams(vmem_limit_bytes=None),
         cost_estimate=estimate(10**9),
         name="second_layer",
     )(core, own, other, bias_a, counts, count, weight, their_weight, bias_b)
@@ -224,7 +228,7 @@
 def plan_of(n_dom):
     if n_dom != 16:
         return None
-    return n_dom // 8, (8, 13, 0, 1), (4, 5, 9, 12)
+    return n_dom // 8, (8, 13, 0), (1, 4, 5, 9, 12)
 
 
 def shards(

time: 75.9 us -> 74.6 us (0.983)
  Pallas kernels: 37.4 us -> 29.4 us
  local copies, waits for them, and re-layouts: 3.54 us -> 8.25 us
  waiting for transfers between devices: 11.2 us -> 13.3 us
    pallas_call x2, Pallas kernels: 13.2 us -> 8.4 us  [first_layer(): pl.pallas_call(body, grid=(total // block,), in_specs=specs, out_specs=ou...]
    unnamed x32 -> x38, local copies, waits for them, and re-layouts: 2.95 us -> 7.66 us
    pallas_call x2, Pallas kernels: 13.3 us -> 10.1 us  [pick_rows(): pl.pallas_call(body, grid=(nodes // block,), in_specs=[pl.BlockSpec(memor...]
    ppermute x8, waiting for transfers between devices: 5.55 us -> 7.29 us  [trade(): return lax.ppermute(found[base], ('dom', 'mp'), pairs)]
  transfers between devices with their start and end apart: 13 -> 13, of which waited for: 4 -> 3; matrix products, arithmetic and copies ran while one was open for 2% -> 1% of each run, Pallas kernels for 35% -> 28%
where the time goes in v3:
time: 74.6 us; the launch traced here: 74.1 us
  Pallas kernels  29.4 us (39%)
  starting transfers between devices  22.9 us (31%)
  waiting for transfers between devices  13.3 us (18%)
  local copies, waits for them, and re-layouts  8.25 us (11%)
    ppermute x8, starting transfers between devices, trade(): return lax.ppermute(found[base], ('dom', 'mp'), pairs)  14.3 us
    pallas_call x2, Pallas kernels, pick_rows(): pl.pallas_call(body, grid=(nodes // block,), in_specs=[pl.BlockSpec(memor...  10.1 us
    pallas_call x2, Pallas kernels, first_layer(): pl.pallas_call(body, grid=(total // block,), in_specs=specs, out_specs=ou...  8.4 us
    unnamed x38, local copies, waits for them, and re-layouts  7.66 us
    ppermute x8, waiting for transfers between devices, trade(): return lax.ppermute(found[base], ('dom', 'mp'), pairs)  7.29 us
    all_to_all x1, starting transfers between devices, shards(): lax.all_to_all(requests[0], 'dom', split_axis=0, concat_axis=0, tiled=True)  6.66 us
    pallas_call x2, Pallas kernels, count_matrices(): pl.pallas_call(body, grid=(total // block,), in_specs=[pl.BlockSpec(memor...  6.58 us
    pallas_call x1, Pallas kernels, second_layer(): pl.pallas_call(body, in_specs=[pl.BlockSpec(memory_space=pltpu.SMEM)] + [...  4.32 us
  transfers between devices with their start and end apart: 13, of which 3 were waited for; matrix products, arithmetic and copies ran while one was open for 1% of the time, Pallas kernels for 28%

profile of v3, /device:TPU:9, one launch (start us, length us, event | category | flops | bytes accessed | tf_op | source)
XLA Modules:
  0.0 74.1 jit_solution(9746350418488140419)
XLA Ops:
  0.0 0.7 collective-permute-start
  0.7 6.7 %all-to-all-start = ((s32[16,1,128]{2,1,0:T(1,128)}), s32[16,1,128]{2,1,0:T(1,128)S(1)}, u32[]{:S(2)}, u32[]{:S(2)}) async-start(s32[16,1,128]{2,1,0:T(1,128)} %bitcast.16), calls=%async_computation | async-start | bytes 16384 | tf_op jit(solution)/shard_map/all_to_all | solution.py:272
  8.1 4.3 %all-to-all-done = s32[16,1,128]{2,1,0:T(1,128)S(1)} async-done(((s32[16,1,128]{2,1,0:T(1,128)}), s32[16,1,128]{2,1,0:T(1,128)S(1)}, u32[]{:S(2)}, u32[]{:S(2)}) %all-to-all-start) | async-done | bytes 8224 | tf_op jit(solution)/shard_map/all_to_all | solution.py:272
  12.3 1.9 %copy-done.1 = bf16[4096,384]{1,0:T(8,128)(2,1)S(1)} copy-done((bf16[4096,384]{1,0:T(8,128)(2,1)S(1)}, bf16[4096,384]{1,0:T(8,128)(2,1)}, u32[]{:S(2)}) %copy-start.1) | copy-done | bytes 3145752
  14.2 3.4 %shard_map.120 = (bf16[128,768]{1,0:T(8,128)(2,1)}, bf16[128,768]{1,0:T(8,128)(2,1)}) custom-call(s32[2]{0:T(128)S(1)} %pad_add_fusion.me_ref.at_ref, s32[16,128]{1,0:T(8,128)S(1)} %bitcast.11, bf16[4096,384]{1,0:T(8,128)(2,1)S(1)} %copy-done.1, bf16[4096,384]{1,0:T(8,128)(2,1)S(1)} %collective-permute-done.their_ref), custom_call_target="tpu_custom_call" | custom-call | flops 1610612736 | bytes 10000000 | tf_op jit(solution)/shard_map/pallas_call | solution.py:112
  18.0 3.0 %collective-permute-start.7 = (bf16[128,768]{1,0:T(8,128)(2,1)}, bf16[128,768]{1,0:T(8,128)(2,1)S(1)}, u32[]{:S(2)}, u32[]{:S(2)}) collective-permute-start(bf16[128,768]{1,0:T(8,128)(2,1)} %get-tuple-element.32), channel_id=1, source_target_pairs={{0,26},{1,31},{2,24},{3,29},{4,30},{5,27},{6,28},{7,25},{8,18},{9,... | collective-permute-start | bytes 589832 | tf_op jit(solution)/shard_map/ppermute | solution.py:297
  21.0 6.7 %shard_map.119 = (bf16[128,768]{1,0:T(8,128)(2,1)}, bf16[128,768]{1,0:T(8,128)(2,1)S(1)}, bf16[128,768]{1,0:T(8,128)(2,1)S(1)}, bf16[128,768]{1,0:T(8,128)(2,1)S...) custom-call(s32[2]{0:T(128)S(1)} %pad_add_fusion.me_ref.at_ref, s32[16,128]{1,0:T(8,128)S(1)} %bitcast.12, ...), custom_call_target="tpu_custom_call" | custom-call | flops 4831838208 | bytes 10000000 | tf_op jit(solution)/shard_map/pallas_call | solution.py:112
  28.4 0.7 copy-done.9
  31.1 2.3 %collective-permute-start.8 = (bf16[128,768]{1,0:T(8,128)(2,1)}, bf16[128,768]{1,0:T(8,128)(2,1)S(1)}, u32[]{:S(2)}, u32[]{:S(2)}) collective-permute-start(bf16[128,768]{1,0:T(8,128)(2,1)} %get-tuple-element.33), channel_id=1, source_target_pairs={{0,0},{1,5},{2,2},{3,7},{4,4},{5,1},{6,6},{7,3},{8,8},{9,13},{10,1... | collective-permute-start | bytes 589832 | tf_op jit(solution)/shard_map/ppermute | solution.py:297
  33.4 2.2 %shard_map.121.c_ref = bf16[2,1024,256]{2,1,0:T(8,128)(2,1)} custom-call(s32[2]{0:T(128)} %copy-done.6, s32[5,256]{1,0:T(8,128)} %bitcast.21, s32[1,256]{1,0:T(1,128)} %bitcast.23, s32[1,256]{1,0:T(1,128)} %bitcast.18), custom_call_target="tpu_custom_call" | custom-call | flops 1000000000 | bytes 10000000 | tf_op jit(solution)/shard_map/pallas_call | solution.py:63
  35.6 2.1 %collective-permute-start.1 = (bf16[128,768]{1,0:T(8,128)(2,1)S(1)}, bf16[128,768]{1,0:T(8,128)(2,1)S(1)}, u32[]{:S(2)}, u32[]{:S(2)}) collective-permute-start(bf16[128,768]{1,0:T(8,128)(2,1)S(1)} %copy-done.16), channel_id=1, source_target_pairs={{0,2},{1,7},{2,0},{3,5},{4,6},{5,3},{6,4},{7,1},{8,10},{9,15},{10,... | collective-permute-start | bytes 589832 | tf_op jit(solution)/shard_map/ppermute | solution.py:297
  37.7 1.2 %collective-permute-start.2 = (bf16[128,768]{1,0:T(8,128)(2,1)S(1)}, bf16[128,768]{1,0:T(8,128)(2,1)S(1)}, u32[]{:S(2)}, u32[]{:S(2)}) collective-permute-start(bf16[128,768]{1,0:T(8,128)(2,1)S(1)} %copy-done.14), channel_id=1, source_target_pairs={{0,8},{1,13},{2,10},{3,15},{4,12},{5,9},{6,14},{7,11},{8,0},{9,5},... | collective-permute-start | bytes 589832 | tf_op jit(solution)/shard_map/ppermute | solution.py:297
  38.9 1.2 %collective-permute-start.3 = (bf16[128,768]{1,0:T(8,128)(2,1)S(1)}, bf16[128,768]{1,0:T(8,128)(2,1)S(1)}, u32[]{:S(2)}, u32[]{:S(2)}) collective-permute-start(bf16[128,768]{1,0:T(8,128)(2,1)S(1)} %copy-done.12), channel_id=1, source_target_pairs={{0,10},{1,15},{2,8},{3,13},{4,14},{5,11},{6,12},{7,9},{8,2},{9,7},... | collective-permute-start | bytes 589832 | tf_op jit(solution)/shard_map/ppermute | solution.py:297
  40.1 2.1 %collective-permute-start.4 = (bf16[128,768]{1,0:T(8,128)(2,1)S(1)}, bf16[128,768]{1,0:T(8,128)(2,1)S(1)}, u32[]{:S(2)}, u32[]{:S(2)}) collective-permute-start(bf16[128,768]{1,0:T(8,128)(2,1)S(1)} %copy-done.10), channel_id=1, source_target_pairs={{0,18},{1,23},{2,16},{3,21},{4,22},{5,19},{6,20},{7,17},{8,26},{9,... | collective-permute-start | bytes 589832 | tf_op jit(solution)/shard_map/ppermute | solution.py:297
  42.2 2.1 %collective-permute-start.5 = (bf16[128,768]{1,0:T(8,128)(2,1)S(1)}, bf16[128,768]{1,0:T(8,128)(2,1)S(1)}, u32[]{:S(2)}, u32[]{:S(2)}) collective-permute-start(bf16[128,768]{1,0:T(8,128)(2,1)S(1)} %copy-done.8), channel_id=1, source_target_pairs={{0,24},{1,29},{2,26},{3,31},{4,28},{5,25},{6,30},{7,27},{8,16},{9,... | collective-permute-start | bytes 589832 | tf_op jit(solution)/shard_map/ppermute | solution.py:297
  44.3 4.4 %shard_map.118 = (bf16[2,384,1024]{2,1,0:T(8,128)(2,1)}, bf16[2,640,1024]{2,1,0:T(8,128)(2,1)}) custom-call(s32[2]{0:T(128)} %copy-done.6, s32[10,1024]{1,0:T(8,128)} %bitcast.20, s32[1,1024]{1,0:T(1,128)} %bitcast.22, s32[1,1024]{1,0:T(1,128)} %bitcast.13), custom_call_target="tpu_custom_call" | custom-call | flops 1000000000 | bytes 10000000 | tf_op jit(solution)/shard_map/pallas_call | solution.py:63
  48.7 1.4 %copy-done.4 = bf16[2,384,1024]{2,1,0:T(8,128)(2,1)S(1)} copy-done((bf16[2,384,1024]{2,1,0:T(8,128)(2,1)S(1)}, bf16[2,384,1024]{2,1,0:T(8,128)(2,1)}, u32[]{:S(2)}) %copy-start.4) | copy-done | bytes 1572888
  50.1 3.8 %shard_map.122.refs_7_ = f32[512,1024]{1,0:T(8,128)S(1)} custom-call(s32[1]{0:T(128)} %bitcast.core_ref, bf16[2,384,1024]{2,1,0:T(8,128)(2,1)S(1)} %copy-done.4, s32[1,1024]{1,0:T(1,128)S(1)} %bitcast.14, bf16[128,768]{1,0:T(8,128)(2,1)S(1)} %collective-permute-done.6.refs_0_, bf16[128,768]{1,0:T(8,128)(2,1)S(1)} %collective-permute-done.7.refs_1_, ...), custom_call_target="tpu_custom_call" | custom-call | flops 1207959552 | bytes 10000000 | tf_op jit(solution)/shard_map/pallas_call | solution.py:179
  53.9 7.3 %collective-permute-done.5.refs_4_ = bf16[128,768]{1,0:T(8,128)(2,1)S(1)} collective-permute-done((bf16[128,768]{1,0:T(8,128)(2,1)S(1)}, bf16[128,768]{1,0:T(8,128)(2,1)S(1)}, u32[]{:S(2)}, u32[]{:S(2)}) %collective-permute-start.5) | collective-permute-done | bytes 196640 | tf_op jit(solution)/shard_map/ppermute | solution.py:297
  61.2 4.6 %shard_map.123.own_ref = bf16[512,1024]{1,0:T(8,128)(2,1)S(1)} custom-call(s32[1]{0:T(128)} %bitcast.core_ref, bf16[2,640,1024]{2,1,0:T(8,128)(2,1)S(1)} %copy-done.3, s32[1,1024]{1,0:T(1,128)S(1)} %bitcast.15, bf16[128,768]{1,0:T(8,128)(2,1)S(1)} %collective-permute-done.1.refs_0_, bf16[128,768]{1,0:T(8,128)(2,1)S(1)} %collective-permute-done.2.refs_1_, ...), custom_call_target="tpu_custom_call" | custom-call | flops 2013265920 | bytes 10000000 | tf_op jit(solution)/shard_map/pallas_call | solution.py:179
  65.8 0.7 collective-permute-start.11
  67.1 1.7 %collective-permute-done.11.other_ref = bf16[512,1024]{1,0:T(8,128)(2,1)S(1)} collective-permute-done((bf16[512,1024]{1,0:T(8,128)(2,1)S(1)}, bf16[512,1024]{1,0:T(8,128)(2,1)S(1)}, u32[]{:S(2)}, u32[]{:S(2)}) %collective-permute-start.11) | collective-permute-done | bytes 1048608 | tf_op jit(solution)/shard_map/ppermute | solution.py:310
  68.8 1.0 %copy-done.17 = bf16[512,1024]{1,0:T(8,128)(2,1)} copy-done((bf16[512,1024]{1,0:T(8,128)(2,1)}, bf16[512,1024]{1,0:T(8,128)(2,1)S(1)}, u32[]{:S(2)}) %copy-start.17) | copy-done | bytes 1048600
  69.8 4.3 %second_layer.1 = bf16[256,256]{1,0:T(8,128)(2,1)} custom-call(s32[1]{0:T(128)} %bitcast.core_ref, bf16[512,1024]{1,0:T(8,128)(2,1)} %copy-done, bf16[512,1024]{1,0:T(8,128)(2,1)} %copy-done.17, f32[1,512]{1,0:T(1,128)} %bitcast.17, bf16[2,1024,256]{2,1,0:T(8,128)(2,1)} %shard_map.121.c_ref, s32[1,256]{1,0:T(1,128)} %bitcast.19, bf16[1024,256]{1,0:T(8,128)(2,1)} %w_ref.1, ...), custom_call_target="tpu_custom_call" | custom-call | flops 1000000000 | bytes 10000000 | tf_op jit(solution)/shard_map/second_layer/pallas_call | solution.py:218
  (49 shorter events, 4.4 us)
Async XLA Ops:
  0.0 8.1 %collective-permute-start = (bf16[4096,384]{1,0:T(8,128)(2,1)}, bf16[4096,384]{1,0:T(8,128)(2,1)S(1)}, u32[]{:S(2)}, u32[]{:S(2)}) collective-permute-start(bf16[4096,384]{1,0:T(8,128)(2,1)} %mine_ref.3), channel_id=1, source_target_pairs={{0,1},{1,0},{2,3},{3,2},{4,5},{5,4},{6,7},{7,6},{8,9},{9,8},{10,11... | collective-permute-start | bytes 9437192 | tf_op jit(solution)/shard_map/ppermute | solution.py:271
  0.7 11.7 %all-to-all-start = ((s32[16,1,128]{2,1,0:T(1,128)}), s32[16,1,128]{2,1,0:T(1,128)S(1)}, u32[]{:S(2)}, u32[]{:S(2)}) async-start(s32[16,1,128]{2,1,0:T(1,128)} %bitcast.16), calls=%async_computation | async-start | bytes 16384 | tf_op jit(solution)/shard_map/all_to_all | solution.py:272
  7.3 30.4 %collective-permute-start.9 = (bf16[1536,256]{1,0:T(8,128)(2,1)}, bf16[1536,256]{1,0:T(8,128)(2,1)}, u32[]{:S(2)}, u32[]{:S(2)}) collective-permute-start(bf16[1536,256]{1,0:T(8,128)(2,1)} %refs_5_.1), channel_id=1, source_target_pairs={{0,1},{1,0},{2,3},{3,2},{4,5},{5,4},{6,7},{7,6},{8,9},{9,8},{10,11... | collective-permute-start | bytes 2359304 | tf_op jit(solution)/shard_map/ppermute | solution.py:302
  7.9 27.6 %collective-permute-start.10 = (bf16[1024,256]{1,0:T(8,128)(2,1)}, bf16[1024,256]{1,0:T(8,128)(2,1)}, u32[]{:S(2)}, u32[]{:S(2)}) collective-permute-start(bf16[1024,256]{1,0:T(8,128)(2,1)} %w_ref.1), channel_id=1, source_target_pairs={{0,1},{1,0},{2,3},{3,2},{4,5},{5,4},{6,7},{7,6},{8,9},{9,8},{10,11... | collective-permute-start | bytes 1572872 | tf_op jit(solution)/shard_map/ppermute | solution.py:303
  8.1 12.9 %copy-start.6 = (s32[2]{0:T(128)}, s32[2]{0:T(128)S(1)}, u32[]{:S(2)}) copy-start(s32[2]{0:T(128)S(1)} %pad_add_fusion.me_ref.at_ref) | copy-start | bytes 28
  17.7 21.2 %collective-permute-start.6 = (bf16[128,768]{1,0:T(8,128)(2,1)}, bf16[128,768]{1,0:T(8,128)(2,1)S(1)}, u32[]{:S(2)}, u32[]{:S(2)}) collective-permute-start(bf16[128,768]{1,0:T(8,128)(2,1)} %get-tuple-element.31), channel_id=1, source_target_pairs={{0,16},{1,21},{2,18},{3,23},{4,20},{5,17},{6,22},{7,19},{8,24},{9,... | collective-permute-start | bytes 589832 | tf_op jit(solution)/shard_map/ppermute | solution.py:297
  18.0 22.1 %collective-permute-start.7 = (bf16[128,768]{1,0:T(8,128)(2,1)}, bf16[128,768]{1,0:T(8,128)(2,1)S(1)}, u32[]{:S(2)}, u32[]{:S(2)}) collective-permute-start(bf16[128,768]{1,0:T(8,128)(2,1)} %get-tuple-element.32), channel_id=1, source_target_pairs={{0,26},{1,31},{2,24},{3,29},{4,30},{5,27},{6,28},{7,25},{8,18},{9,... | collective-permute-start | bytes 589832 | tf_op jit(solution)/shard_map/ppermute | solution.py:297
  31.0 4.5 %copy-start.16 = (bf16[128,768]{1,0:T(8,128)(2,1)S(1)}, bf16[128,768]{1,0:T(8,128)(2,1)}, u32[]{:S(2)}) copy-start(bf16[128,768]{1,0:T(8,128)(2,1)} %copy-done.15) | copy-start | bytes 589828
  31.0 6.7 %copy-start.14 = (bf16[128,768]{1,0:T(8,128)(2,1)S(1)}, bf16[128,768]{1,0:T(8,128)(2,1)}, u32[]{:S(2)}) copy-start(bf16[128,768]{1,0:T(8,128)(2,1)} %copy-done.13) | copy-start | bytes 589828
  31.0 7.9 %copy-start.12 = (bf16[128,768]{1,0:T(8,128)(2,1)S(1)}, bf16[128,768]{1,0:T(8,128)(2,1)}, u32[]{:S(2)}) copy-start(bf16[128,768]{1,0:T(8,128)(2,1)} %copy-done.11) | copy-start | bytes 589828
  31.0 9.1 %copy-start.10 = (bf16[128,768]{1,0:T(8,128)(2,1)S(1)}, bf16[128,768]{1,0:T(8,128)(2,1)}, u32[]{:S(2)}) copy-start(bf16[128,768]{1,0:T(8,128)(2,1)} %copy-done.9) | copy-start | bytes 589828
  31.1 11.1 %copy-start.8 = (bf16[128,768]{1,0:T(8,128)(2,1)S(1)}, bf16[128,768]{1,0:T(8,128)(2,1)}, u32[]{:S(2)}) copy-start(bf16[128,768]{1,0:T(8,128)(2,1)} %copy-done.7) | copy-start | bytes 589828
  31.1 11.1 %collective-permute-start.8 = (bf16[128,768]{1,0:T(8,128)(2,1)}, bf16[128,768]{1,0:T(8,128)(2,1)S(1)}, u32[]{:S(2)}, u32[]{:S(2)}) collective-permute-start(bf16[128,768]{1,0:T(8,128)(2,1)} %get-tuple-element.33), channel_id=1, source_target_pairs={{0,0},{1,5},{2,2},{3,7},{4,4},{5,1},{6,6},{7,3},{8,8},{9,13},{10,1... | collective-permute-start | bytes 589832 | tf_op jit(solution)/shard_map/ppermute | solution.py:297
  35.5 13.1 %copy-start.2 = (bf16[1536,256]{1,0:T(8,128)(2,1)S(1)}, bf16[1536,256]{1,0:T(8,128)(2,1)}, u32[]{:S(2)}) copy-start(bf16[1536,256]{1,0:T(8,128)(2,1)} %refs_5_.1) | copy-start | bytes 2359300
  35.5 13.1 %copy-start.5 = (s32[1024]{0:T(1024)S(1)}, s32[1024]{0:T(1024)}, u32[]{:S(2)}) copy-start(s32[1024]{0:T(1024)} %param.20) | copy-start | bytes 12292
  35.6 18.3 %collective-permute-start.1 = (bf16[128,768]{1,0:T(8,128)(2,1)S(1)}, bf16[128,768]{1,0:T(8,128)(2,1)S(1)}, u32[]{:S(2)}, u32[]{:S(2)}) collective-permute-start(bf16[128,768]{1,0:T(8,128)(2,1)S(1)} %copy-done.16), channel_id=1, source_target_pairs={{0,2},{1,7},{2,0},{3,5},{4,6},{5,3},{6,4},{7,1},{8,10},{9,15},{10,... | collective-permute-start | bytes 589832 | tf_op jit(solution)/shard_map/ppermute | solution.py:297
  37.7 16.2 %collective-permute-start.2 = (bf16[128,768]{1,0:T(8,128)(2,1)S(1)}, bf16[128,768]{1,0:T(8,128)(2,1)S(1)}, u32[]{:S(2)}, u32[]{:S(2)}) collective-permute-start(bf16[128,768]{1,0:T(8,128)(2,1)S(1)} %copy-done.14), channel_id=1, source_target_pairs={{0,8},{1,13},{2,10},{3,15},{4,12},{5,9},{6,14},{7,11},{8,0},{9,5},... | collective-permute-start | bytes 589832 | tf_op jit(solution)/shard_map/ppermute | solution.py:297
  38.9 15.0 %collective-permute-start.3 = (bf16[128,768]{1,0:T(8,128)(2,1)S(1)}, bf16[128,768]{1,0:T(8,128)(2,1)S(1)}, u32[]{:S(2)}, u32[]{:S(2)}) collective-permute-start(bf16[128,768]{1,0:T(8,128)(2,1)S(1)} %copy-done.12), channel_id=1, source_target_pairs={{0,10},{1,15},{2,8},{3,13},{4,14},{5,11},{6,12},{7,9},{8,2},{9,7},... | collective-permute-start | bytes 589832 | tf_op jit(solution)/shard_map/ppermute | solution.py:297
  40.1 13.8 %collective-permute-start.4 = (bf16[128,768]{1,0:T(8,128)(2,1)S(1)}, bf16[128,768]{1,0:T(8,128)(2,1)S(1)}, u32[]{:S(2)}, u32[]{:S(2)}) collective-permute-start(bf16[128,768]{1,0:T(8,128)(2,1)S(1)} %copy-done.10), channel_id=1, source_target_pairs={{0,18},{1,23},{2,16},{3,21},{4,22},{5,19},{6,20},{7,17},{8,26},{9,... | collective-permute-start | bytes 589832 | tf_op jit(solution)/shard_map/ppermute | solution.py:297
  42.2 19.0 %collective-permute-start.5 = (bf16[128,768]{1,0:T(8,128)(2,1)S(1)}, bf16[128,768]{1,0:T(8,128)(2,1)S(1)}, u32[]{:S(2)}, u32[]{:S(2)}) collective-permute-start(bf16[128,768]{1,0:T(8,128)(2,1)S(1)} %copy-done.8), channel_id=1, source_target_pairs={{0,24},{1,29},{2,26},{3,31},{4,28},{5,25},{6,30},{7,27},{8,16},{9,... | collective-permute-start | bytes 589832 | tf_op jit(solution)/shard_map/ppermute | solution.py:297
  50.1 11.1 %copy-start.3 = (bf16[2,640,1024]{2,1,0:T(8,128)(2,1)S(1)}, bf16[2,640,1024]{2,1,0:T(8,128)(2,1)}, u32[]{:S(2)}) copy-start(bf16[2,640,1024]{2,1,0:T(8,128)(2,1)} %get-tuple-element.24.c_ref) | copy-start | bytes 7864324
  61.2 5.4 %copy-start.18 = (f32[512]{0:T(512)S(1)}, f32[512]{0:T(512)}, u32[]{:S(2)}) copy-start(f32[512]{0:T(512)} %param.16) | copy-start | bytes 6148
  65.8 3.0 %copy-start = (bf16[512,1024]{1,0:T(8,128)(2,1)}, bf16[512,1024]{1,0:T(8,128)(2,1)S(1)}, u32[]{:S(2)}) copy-start(bf16[512,1024]{1,0:T(8,128)(2,1)S(1)} %shard_map.123.own_ref) | copy-start | bytes 3145732
  65.8 3.0 %collective-permute-start.11 = (bf16[512,1024]{1,0:T(8,128)(2,1)S(1)}, bf16[512,1024]{1,0:T(8,128)(2,1)S(1)}, u32[]{:S(2)}, u32[]{:S(2)}) collective-permute-start(bf16[512,1024]{1,0:T(8,128)(2,1)S(1)} %shard_map.123.own_ref), channel_id=1, source_target_pairs={{0,1},{1,0},{2,3},{3,2},{4,5},{5,4},{6,7},{7,6},{8,9},{9,8},{10,11... | collective-permute-start | bytes 3145736 | tf_op jit(solution)/shard_map/ppermute | solution.py:310
  (8 other events, 7.6 us)

commit v4 on v3

--- a/solution.py
+++ b/solution.py
@@ -9,7 +9,8 @@
 
 
 LANES = 128
-PICK = 2048
+TAIL = 4
+PICK = 4096
 BATCHES = ((8, 13), (0, 1, 4, 5, 9, 12))
 
 
@@ -131,7 +132,7 @@
     cols = rows[0].shape[1]
     features, half = weight.shape[0] // 2, weight.shape[1]
     share = cols if cols < features else features // 2
-    block = min(4 * LANES, total)
+    block = min(8 * LANES, total)
     have = before is not None
 
     def body(core_ref, c_ref, n_ref, *refs):
@@ -189,37 +190,56 @@
 
 
 def second_layer(own, other, bias_a, counts, count, core, weight, their_weight, bias_b):
-    hidden, _ = own.shape
+    hidden, hops = own.shape
     half = hidden // 2
     seeds = counts.shape[2]
-
-    def body(core_ref, own_ref, other_ref, ba_ref, c_ref, n_ref, w_ref, t_ref, bb_ref, o_ref):
-        bias = jnp.broadcast_to(ba_ref[...], (LANES, hidden)).T[:, :1]
-        value = own_ref[...].astype(jnp.float32) + other_ref[...].astype(jnp.float32) + bias
+    block = min(TAIL * LANES, hops)
+
+    def body(core_ref, own_ref, other_ref, ba_ref, c_ref, n_ref, w_ref, t_ref, bb_ref, o_ref, acc, bias):
+        now = pl.program_id(0)
+
+        @pl.when(now == 0)
+        def _():
+            bias[...] = jnp.broadcast_to(ba_ref[...], (LANES, hidden)).T
+            acc[...] = jnp.zeros_like(acc)
+
+        value = own_ref[...].astype(jnp.float32) + other_ref[...].astype(jnp.float32) + bias[:, :1]
         value = jnp.maximum(value, 0.0).astype(jnp.bfloat16)
-        self_b = jnp.dot(value, c_ref[1], preferred_element_type=jnp.float32)
-        mean_b = jnp.dot(value, c_ref[0], preferred_element_type=jnp.float32)
-        mean_b = mean_b * (1.0 / n_ref[...].astype(jnp.float32))
-        self_b = self_b.T.astype(jnp.bfloat16)
-        mean_b = mean_b.T.astype(jnp.bfloat16)
-
-        def state_of(ref, index):
-            state = jnp.dot(self_b, ref[:hidden, :], preferred_element_type=jnp.float32)
-            state = state + jnp.dot(mean_b, ref[hidden:, :], preferred_element_type=jnp.float32)
-            return jnp.maximum(state + bb_ref[pl.ds(index, 1), :], 0.0)
-
-        state = state_of(w_ref, core_ref[0])
-        theirs = state_of(t_ref, 1 - core_ref[0])
-        squares = jnp.sum(state * state + theirs * theirs, axis=1, keepdims=True)
-        scale = jnp.sqrt(jnp.float32(hidden)) / jnp.sqrt(squares + hidden)
-        o_ref[...] = (state * scale).astype(jnp.bfloat16)
-
-    whole = pl.BlockSpec(memory_space=pltpu.VMEM)
+        acc[0] += jnp.dot(value, c_ref[0], preferred_element_type=jnp.float32)
+        acc[1] += jnp.dot(value, c_ref[1], preferred_element_type=jnp.float32)
+
+        @pl.when(now == pl.num_programs(0) - 1)
+        def _():
+            self_b = acc[1].astype(jnp.bfloat16).T
+            mean_b = (acc[0] * (1.0 / n_ref[...].astype(jnp.float32))).astype(jnp.bfloat16).T
+
+            def state_of(ref, index):
+                state = jnp.dot(self_b, ref[:hidden, :], preferred_element_type=jnp.float32)
+                state = state + jnp.dot(mean_b, ref[hidden:, :], preferred_element_type=jnp.float32)
+                return jnp.maximum(state + bb_ref[pl.ds(index, 1), :], 0.0)
+
+            state = state_of(w_ref, core_ref[0])
+            theirs = state_of(t_ref, 1 - core_ref[0])
+            squares = jnp.sum(state * state + theirs * theirs, axis=1, keepdims=True)
+            scale = jnp.sqrt(jnp.float32(hidden)) / jnp.sqrt(squares + hidden)
+            o_ref[...] = (state * scale).astype(jnp.bfloat16)
+
+    share = pl.BlockSpec((hidden, block), lambda i: (0, i))
+    whole = [pl.BlockSpec(value.shape, lambda i: (0, 0)) for value in (count, weight, their_weight, bias_b)]
     return pl.pallas_call(
         body,
-        in_specs=[pl.BlockSpec(memory_space=pltpu.SMEM)] + [whole] * 8,
+        grid=(hops // block,),
+        in_specs=[
+            pl.BlockSpec(memory_space=pltpu.SMEM),
+            share,
+            share,
+            pl.BlockSpec(bias_a.shape, lambda i: (0, 0)),
+            pl.BlockSpec((2, block, seeds), lambda i: (0, i, 0)),
+            *whole,
+        ],
+        out_specs=pl.BlockSpec((seeds, half), lambda i: (0, 0)),
         out_shape=jax.ShapeDtypeStruct((seeds, half), jnp.bfloat16),
-        compiler_params=pltpu.CompilerParams(vmem_limit_bytes=None),
+        scratch_shapes=[pltpu.VMEM((2, hidden, seeds), jnp.float32), pltpu.VMEM((hidden, LANES), jnp.float32)],
         cost_estimate=estimate(10**9),
         name="second_layer",
     )(core, own, other, bias_a, counts, count, weight, their_weight, bias_b)

time: 74.6 us -> 73.1 us (0.980)
  Pallas kernels: 29.4 us -> 27.5 us
    pallas_call x2, Pallas kernels: 10.1 us -> 9.22 us  [pick_rows(): pl.pallas_call(body, grid=(nodes // block,), in_specs=[pl.BlockSpec(memor...]
    pallas_call x2, Pallas kernels: 8.4 us -> 7.54 us  [first_layer(): pl.pallas_call(body, grid=(total // block,), in_specs=specs, out_specs=ou...]
  transfers between devices with their start and end apart: 13 -> 13, of which waited for: 3 -> 3; matrix products, arithmetic and copies ran while one was open for 1% -> 1% of each run, Pallas kernels for 28% -> 26%
where the time goes in v4:
time: 73.1 us; the launch traced here: 72.6 us
  Pallas kernels  27.5 us (38%)
  starting transfers between devices  23 us (31%)
  waiting for transfers between devices  13.7 us (19%)
  local copies, waits for them, and re-layouts  8.25 us (11%)
    ppermute x8, starting transfers between devices, trade(): return lax.ppermute(found[base], ('dom', 'mp'), pairs)  14.3 us
    pallas_call x2, Pallas kernels, pick_rows(): pl.pallas_call(body, grid=(nodes // block,), in_specs=[pl.BlockSpec(memor...  9.22 us
    ppermute x8, waiting for transfers between devices, trade(): return lax.ppermute(found[base], ('dom', 'mp'), pairs)  7.71 us
    unnamed x38, local copies, waits for them, and re-layouts  7.66 us
    pallas_call x2, Pallas kernels, first_layer(): pl.pallas_call(body, grid=(total // block,), in_specs=specs, out_specs=ou...  7.54 us
    all_to_all x1, starting transfers between devices, shards(): lax.all_to_all(requests[0], 'dom', split_axis=0, concat_axis=0, tiled=True)  6.66 us
    pallas_call x2, Pallas kernels, count_matrices(): pl.pallas_call(body, grid=(total // block,), in_specs=[pl.BlockSpec(memor...  6.58 us
    all_to_all x1, waiting for transfers between devices, shards(): lax.all_to_all(requests[0], 'dom', split_axis=0, concat_axis=0, tiled=True)  4.28 us
  transfers between devices with their start and end apart: 13, of which 3 were waited for; matrix products, arithmetic and copies ran while one was open for 1% of the time, Pallas kernels for 26%

profile of v4, /device:TPU:9, one launch (start us, length us, event | category | flops | bytes accessed | tf_op | source)
XLA Modules:
  0.0 72.6 jit_solution(863755157402109997)
XLA Ops:
  0.0 0.7 collective-permute-start
  0.7 6.7 %all-to-all-start = ((s32[16,1,128]{2,1,0:T(1,128)}), s32[16,1,128]{2,1,0:T(1,128)S(1)}, u32[]{:S(2)}, u32[]{:S(2)}) async-start(s32[16,1,128]{2,1,0:T(1,128)} %bitcast.16), calls=%async_computation | async-start | bytes 16384 | tf_op jit(solution)/shard_map/all_to_all | solution.py:292
  8.1 4.3 %all-to-all-done = s32[16,1,128]{2,1,0:T(1,128)S(1)} async-done(((s32[16,1,128]{2,1,0:T(1,128)}), s32[16,1,128]{2,1,0:T(1,128)S(1)}, u32[]{:S(2)}, u32[]{:S(2)}) %all-to-all-start) | async-done | bytes 8224 | tf_op jit(solution)/shard_map/all_to_all | solution.py:292
  12.3 1.9 %copy-done.1 = bf16[4096,384]{1,0:T(8,128)(2,1)S(1)} copy-done((bf16[4096,384]{1,0:T(8,128)(2,1)S(1)}, bf16[4096,384]{1,0:T(8,128)(2,1)}, u32[]{:S(2)}) %copy-start.1) | copy-done | bytes 3145752
  14.2 3.1 %shard_map.120 = (bf16[128,768]{1,0:T(8,128)(2,1)}, bf16[128,768]{1,0:T(8,128)(2,1)}) custom-call(s32[2]{0:T(128)S(1)} %pad_add_fusion.me_ref.at_ref, s32[16,128]{1,0:T(8,128)S(1)} %bitcast.11, bf16[4096,384]{1,0:T(8,128)(2,1)S(1)} %copy-done.1, bf16[4096,384]{1,0:T(8,128)(2,1)S(1)} %collective-permute-done.their_ref), custom_call_target="tpu_custom_call" | custom-call | flops 1610612736 | bytes 10000000 | tf_op jit(solution)/shard_map/pallas_call | solution.py:113
  17.7 3.0 %collective-permute-start.7 = (bf16[128,768]{1,0:T(8,128)(2,1)}, bf16[128,768]{1,0:T(8,128)(2,1)S(1)}, u32[]{:S(2)}, u32[]{:S(2)}) collective-permute-start(bf16[128,768]{1,0:T(8,128)(2,1)} %get-tuple-element.32), channel_id=1, source_target_pairs={{0,26},{1,31},{2,24},{3,29},{4,30},{5,27},{6,28},{7,25},{8,18},{9,... | collective-permute-start | bytes 589832 | tf_op jit(solution)/shard_map/ppermute | solution.py:317
  20.6 6.1 %shard_map.119 = (bf16[128,768]{1,0:T(8,128)(2,1)}, bf16[128,768]{1,0:T(8,128)(2,1)S(1)}, bf16[128,768]{1,0:T(8,128)(2,1)S(1)}, bf16[128,768]{1,0:T(8,128)(2,1)S...) custom-call(s32[2]{0:T(128)S(1)} %pad_add_fusion.me_ref.at_ref, s32[16,128]{1,0:T(8,128)S(1)} %bitcast.12, ...), custom_call_target="tpu_custom_call" | custom-call | flops 4831838208 | bytes 10000000 | tf_op jit(solution)/shard_map/pallas_call | solution.py:113
  27.4 0.7 copy-done.9
  30.1 2.3 %collective-permute-start.8 = (bf16[128,768]{1,0:T(8,128)(2,1)}, bf16[128,768]{1,0:T(8,128)(2,1)S(1)}, u32[]{:S(2)}, u32[]{:S(2)}) collective-permute-start(bf16[128,768]{1,0:T(8,128)(2,1)} %get-tuple-element.33), channel_id=1, source_target_pairs={{0,0},{1,5},{2,2},{3,7},{4,4},{5,1},{6,6},{7,3},{8,8},{9,13},{10,1... | collective-permute-start | bytes 589832 | tf_op jit(solution)/shard_map/ppermute | solution.py:317
  32.4 2.2 %shard_map.121.c_ref = bf16[2,1024,256]{2,1,0:T(8,128)(2,1)} custom-call(s32[2]{0:T(128)} %copy-done.6, s32[5,256]{1,0:T(8,128)} %bitcast.21, s32[1,256]{1,0:T(1,128)} %bitcast.23, s32[1,256]{1,0:T(1,128)} %bitcast.18), custom_call_target="tpu_custom_call" | custom-call | flops 1000000000 | bytes 10000000 | tf_op jit(solution)/shard_map/pallas_call | solution.py:64
  34.6 2.1 %collective-permute-start.1 = (bf16[128,768]{1,0:T(8,128)(2,1)S(1)}, bf16[128,768]{1,0:T(8,128)(2,1)S(1)}, u32[]{:S(2)}, u32[]{:S(2)}) collective-permute-start(bf16[128,768]{1,0:T(8,128)(2,1)S(1)} %copy-done.16), channel_id=1, source_target_pairs={{0,2},{1,7},{2,0},{3,5},{4,6},{5,3},{6,4},{7,1},{8,10},{9,15},{10,... | collective-permute-start | bytes 589832 | tf_op jit(solution)/shard_map/ppermute | solution.py:317
  36.8 1.2 %collective-permute-start.2 = (bf16[128,768]{1,0:T(8,128)(2,1)S(1)}, bf16[128,768]{1,0:T(8,128)(2,1)S(1)}, u32[]{:S(2)}, u32[]{:S(2)}) collective-permute-start(bf16[128,768]{1,0:T(8,128)(2,1)S(1)} %copy-done.14), channel_id=1, source_target_pairs={{0,8},{1,13},{2,10},{3,15},{4,12},{5,9},{6,14},{7,11},{8,0},{9,5},... | collective-permute-start | bytes 589832 | tf_op jit(solution)/shard_map/ppermute | solution.py:317
  38.0 1.2 %collective-permute-start.3 = (bf16[128,768]{1,0:T(8,128)(2,1)S(1)}, bf16[128,768]{1,0:T(8,128)(2,1)S(1)}, u32[]{:S(2)}, u32[]{:S(2)}) collective-permute-start(bf16[128,768]{1,0:T(8,128)(2,1)S(1)} %copy-done.12), channel_id=1, source_target_pairs={{0,10},{1,15},{2,8},{3,13},{4,14},{5,11},{6,12},{7,9},{8,2},{9,7},... | collective-permute-start | bytes 589832 | tf_op jit(solution)/shard_map/ppermute | solution.py:317
  39.2 2.1 %collective-permute-start.4 = (bf16[128,768]{1,0:T(8,128)(2,1)S(1)}, bf16[128,768]{1,0:T(8,128)(2,1)S(1)}, u32[]{:S(2)}, u32[]{:S(2)}) collective-permute-start(bf16[128,768]{1,0:T(8,128)(2,1)S(1)} %copy-done.10), channel_id=1, source_target_pairs={{0,18},{1,23},{2,16},{3,21},{4,22},{5,19},{6,20},{7,17},{8,26},{9,... | collective-permute-start | bytes 589832 | tf_op jit(solution)/shard_map/ppermute | solution.py:317
  41.3 2.1 %collective-permute-start.5 = (bf16[128,768]{1,0:T(8,128)(2,1)S(1)}, bf16[128,768]{1,0:T(8,128)(2,1)S(1)}, u32[]{:S(2)}, u32[]{:S(2)}) collective-permute-start(bf16[128,768]{1,0:T(8,128)(2,1)S(1)} %copy-done.8), channel_id=1, source_target_pairs={{0,24},{1,29},{2,26},{3,31},{4,28},{5,25},{6,30},{7,27},{8,16},{9,... | collective-permute-start | bytes 589832 | tf_op jit(solution)/shard_map/ppermute | solution.py:317
  43.3 4.4 %shard_map.118 = (bf16[2,384,1024]{2,1,0:T(8,128)(2,1)}, bf16[2,640,1024]{2,1,0:T(8,128)(2,1)}) custom-call(s32[2]{0:T(128)} %copy-done.6, s32[10,1024]{1,0:T(8,128)} %bitcast.20, s32[1,1024]{1,0:T(1,128)} %bitcast.22, s32[1,1024]{1,0:T(1,128)} %bitcast.13), custom_call_target="tpu_custom_call" | custom-call | flops 1000000000 | bytes 10000000 | tf_op jit(solution)/shard_map/pallas_call | solution.py:64
  47.8 1.4 %copy-done.4 = bf16[2,384,1024]{2,1,0:T(8,128)(2,1)S(1)} copy-done((bf16[2,384,1024]{2,1,0:T(8,128)(2,1)S(1)}, bf16[2,384,1024]{2,1,0:T(8,128)(2,1)}, u32[]{:S(2)}) %copy-start.4) | copy-done | bytes 1572888
  49.2 3.3 %shard_map.122.refs_7_ = f32[512,1024]{1,0:T(8,128)S(1)} custom-call(s32[1]{0:T(128)} %bitcast.core_ref, bf16[2,384,1024]{2,1,0:T(8,128)(2,1)S(1)} %copy-done.4, s32[1,1024]{1,0:T(1,128)S(1)} %bitcast.14, bf16[128,768]{1,0:T(8,128)(2,1)S(1)} %collective-permute-done.6.refs_0_, bf16[128,768]{1,0:T(8,128)(2,1)S(1)} %collective-permute-done.7.refs_1_, ...), custom_call_target="tpu_custom_call" | custom-call | flops 1207959552 | bytes 10000000 | tf_op jit(solution)/shard_map/pallas_call | solution.py:180
  52.6 7.7 %collective-permute-done.5.refs_4_ = bf16[128,768]{1,0:T(8,128)(2,1)S(1)} collective-permute-done((bf16[128,768]{1,0:T(8,128)(2,1)S(1)}, bf16[128,768]{1,0:T(8,128)(2,1)S(1)}, u32[]{:S(2)}, u32[]{:S(2)}) %collective-permute-start.5) | collective-permute-done | bytes 196640 | tf_op jit(solution)/shard_map/ppermute | solution.py:317
  60.3 4.2 %shard_map.123.own_ref = bf16[512,1024]{1,0:T(8,128)(2,1)S(1)} custom-call(s32[1]{0:T(128)} %bitcast.core_ref, bf16[2,640,1024]{2,1,0:T(8,128)(2,1)S(1)} %copy-done.3, s32[1,1024]{1,0:T(1,128)S(1)} %bitcast.15, bf16[128,768]{1,0:T(8,128)(2,1)S(1)} %collective-permute-done.1.refs_0_, bf16[128,768]{1,0:T(8,128)(2,1)S(1)} %collective-permute-done.2.refs_1_, ...), custom_call_target="tpu_custom_call" | custom-call | flops 2013265920 | bytes 10000000 | tf_op jit(solution)/shard_map/pallas_call | solution.py:180
  64.5 0.7 collective-permute-start.11
  65.8 1.7 %collective-permute-done.11.other_ref = bf16[512,1024]{1,0:T(8,128)(2,1)S(1)} collective-permute-done((bf16[512,1024]{1,0:T(8,128)(2,1)S(1)}, bf16[512,1024]{1,0:T(8,128)(2,1)S(1)}, u32[]{:S(2)}, u32[]{:S(2)}) %collective-permute-start.11) | collective-permute-done | bytes 1048608 | tf_op jit(solution)/shard_map/ppermute | solution.py:330
  67.5 1.0 %copy-done.17 = bf16[512,1024]{1,0:T(8,128)(2,1)} copy-done((bf16[512,1024]{1,0:T(8,128)(2,1)}, bf16[512,1024]{1,0:T(8,128)(2,1)S(1)}, u32[]{:S(2)}) %copy-start.17) | copy-done | bytes 1048600
  68.4 4.2 %second_layer.1 = bf16[256,256]{1,0:T(8,128)(2,1)} custom-call(s32[1]{0:T(128)} %bitcast.core_ref, bf16[512,1024]{1,0:T(8,128)(2,1)} %copy-done, bf16[512,1024]{1,0:T(8,128)(2,1)} %copy-done.17, f32[1,512]{1,0:T(1,128)} %bitcast.17, bf16[2,1024,256]{2,1,0:T(8,128)(2,1)} %shard_map.121.c_ref, s32[1,256]{1,0:T(1,128)} %bitcast.19, bf16[1024,256]{1,0:T(8,128)(2,1)} %w_ref.1, ...), custom_call_target="tpu_custom_call" | custom-call | flops 1000000000 | bytes 10000000 | tf_op jit(solution)/shard_map/second_layer/pallas_call | solution.py:229
  (49 shorter events, 4.4 us)
Async XLA Ops:
  0.0 8.1 %collective-permute-start = (bf16[4096,384]{1,0:T(8,128)(2,1)}, bf16[4096,384]{1,0:T(8,128)(2,1)S(1)}, u32[]{:S(2)}, u32[]{:S(2)}) collective-permute-start(bf16[4096,384]{1,0:T(8,128)(2,1)} %mine_ref.3), channel_id=1, source_target_pairs={{0,1},{1,0},{2,3},{3,2},{4,5},{5,4},{6,7},{7,6},{8,9},{9,8},{10,11... | collective-permute-start | bytes 9437192 | tf_op jit(solution)/shard_map/ppermute | solution.py:291
  0.7 11.7 %all-to-all-start = ((s32[16,1,128]{2,1,0:T(1,128)}), s32[16,1,128]{2,1,0:T(1,128)S(1)}, u32[]{:S(2)}, u32[]{:S(2)}) async-start(s32[16,1,128]{2,1,0:T(1,128)} %bitcast.16), calls=%async_computation | async-start | bytes 16384 | tf_op jit(solution)/shard_map/all_to_all | solution.py:292
  7.3 29.4 %collective-permute-start.9 = (bf16[1536,256]{1,0:T(8,128)(2,1)}, bf16[1536,256]{1,0:T(8,128)(2,1)}, u32[]{:S(2)}, u32[]{:S(2)}) collective-permute-start(bf16[1536,256]{1,0:T(8,128)(2,1)} %refs_5_.1), channel_id=1, source_target_pairs={{0,1},{1,0},{2,3},{3,2},{4,5},{5,4},{6,7},{7,6},{8,9},{9,8},{10,11... | collective-permute-start | bytes 2359304 | tf_op jit(solution)/shard_map/ppermute | solution.py:322
  7.9 26.7 %collective-permute-start.10 = (bf16[1024,256]{1,0:T(8,128)(2,1)}, bf16[1024,256]{1,0:T(8,128)(2,1)}, u32[]{:S(2)}, u32[]{:S(2)}) collective-permute-start(bf16[1024,256]{1,0:T(8,128)(2,1)} %w_ref.1), channel_id=1, source_target_pairs={{0,1},{1,0},{2,3},{3,2},{4,5},{5,4},{6,7},{7,6},{8,9},{9,8},{10,11... | collective-permute-start | bytes 1572872 | tf_op jit(solution)/shard_map/ppermute | solution.py:323
  8.1 12.6 %copy-start.6 = (s32[2]{0:T(128)}, s32[2]{0:T(128)S(1)}, u32[]{:S(2)}) copy-start(s32[2]{0:T(128)S(1)} %pad_add_fusion.me_ref.at_ref) | copy-start | bytes 28
  17.3 20.6 %collective-permute-start.6 = (bf16[128,768]{1,0:T(8,128)(2,1)}, bf16[128,768]{1,0:T(8,128)(2,1)S(1)}, u32[]{:S(2)}, u32[]{:S(2)}) collective-permute-start(bf16[128,768]{1,0:T(8,128)(2,1)} %get-tuple-element.31), channel_id=1, source_target_pairs={{0,16},{1,21},{2,18},{3,23},{4,20},{5,17},{6,22},{7,19},{8,24},{9,... | collective-permute-start | bytes 589832 | tf_op jit(solution)/shard_map/ppermute | solution.py:317
  17.7 21.5 %collective-permute-start.7 = (bf16[128,768]{1,0:T(8,128)(2,1)}, bf16[128,768]{1,0:T(8,128)(2,1)S(1)}, u32[]{:S(2)}, u32[]{:S(2)}) collective-permute-start(bf16[128,768]{1,0:T(8,128)(2,1)} %get-tuple-element.32), channel_id=1, source_target_pairs={{0,26},{1,31},{2,24},{3,29},{4,30},{5,27},{6,28},{7,25},{8,18},{9,... | collective-permute-start | bytes 589832 | tf_op jit(solution)/shard_map/ppermute | solution.py:317
  30.1 4.5 %copy-start.16 = (bf16[128,768]{1,0:T(8,128)(2,1)S(1)}, bf16[128,768]{1,0:T(8,128)(2,1)}, u32[]{:S(2)}) copy-start(bf16[128,768]{1,0:T(8,128)(2,1)} %copy-done.15) | copy-start | bytes 589828
  30.1 6.7 %copy-start.14 = (bf16[128,768]{1,0:T(8,128)(2,1)S(1)}, bf16[128,768]{1,0:T(8,128)(2,1)}, u32[]{:S(2)}) copy-start(bf16[128,768]{1,0:T(8,128)(2,1)} %copy-done.13) | copy-start | bytes 589828
  30.1 7.9 %copy-start.12 = (bf16[128,768]{1,0:T(8,128)(2,1)S(1)}, bf16[128,768]{1,0:T(8,128)(2,1)}, u32[]{:S(2)}) copy-start(bf16[128,768]{1,0:T(8,128)(2,1)} %copy-done.11) | copy-start | bytes 589828
  30.1 9.1 %copy-start.10 = (bf16[128,768]{1,0:T(8,128)(2,1)S(1)}, bf16[128,768]{1,0:T(8,128)(2,1)}, u32[]{:S(2)}) copy-start(bf16[128,768]{1,0:T(8,128)(2,1)} %copy-done.9) | copy-start | bytes 589828
  30.1 11.1 %copy-start.8 = (bf16[128,768]{1,0:T(8,128)(2,1)S(1)}, bf16[128,768]{1,0:T(8,128)(2,1)}, u32[]{:S(2)}) copy-start(bf16[128,768]{1,0:T(8,128)(2,1)} %copy-done.7) | copy-start | bytes 589828
  30.1 11.1 %collective-permute-start.8 = (bf16[128,768]{1,0:T(8,128)(2,1)}, bf16[128,768]{1,0:T(8,128)(2,1)S(1)}, u32[]{:S(2)}, u32[]{:S(2)}) collective-permute-start(bf16[128,768]{1,0:T(8,128)(2,1)} %get-tuple-element.33), channel_id=1, source_target_pairs={{0,0},{1,5},{2,2},{3,7},{4,4},{5,1},{6,6},{7,3},{8,8},{9,13},{10,1... | collective-permute-start | bytes 589832 | tf_op jit(solution)/shard_map/ppermute | solution.py:317
  34.6 13.1 %copy-start.2 = (bf16[1536,256]{1,0:T(8,128)(2,1)S(1)}, bf16[1536,256]{1,0:T(8,128)(2,1)}, u32[]{:S(2)}) copy-start(bf16[1536,256]{1,0:T(8,128)(2,1)} %refs_5_.1) | copy-start | bytes 2359300
  34.6 13.1 %copy-start.5 = (s32[1024]{0:T(1024)S(1)}, s32[1024]{0:T(1024)}, u32[]{:S(2)}) copy-start(s32[1024]{0:T(1024)} %param.20) | copy-start | bytes 12292
  34.6 17.9 %collective-permute-start.1 = (bf16[128,768]{1,0:T(8,128)(2,1)S(1)}, bf16[128,768]{1,0:T(8,128)(2,1)S(1)}, u32[]{:S(2)}, u32[]{:S(2)}) collective-permute-start(bf16[128,768]{1,0:T(8,128)(2,1)S(1)} %copy-done.16), channel_id=1, source_target_pairs={{0,2},{1,7},{2,0},{3,5},{4,6},{5,3},{6,4},{7,1},{8,10},{9,15},{10,... | collective-permute-start | bytes 589832 | tf_op jit(solution)/shard_map/ppermute | solution.py:317
  36.8 15.8 %collective-permute-start.2 = (bf16[128,768]{1,0:T(8,128)(2,1)S(1)}, bf16[128,768]{1,0:T(8,128)(2,1)S(1)}, u32[]{:S(2)}, u32[]{:S(2)}) collective-permute-start(bf16[128,768]{1,0:T(8,128)(2,1)S(1)} %copy-done.14), channel_id=1, source_target_pairs={{0,8},{1,13},{2,10},{3,15},{4,12},{5,9},{6,14},{7,11},{8,0},{9,5},... | collective-permute-start | bytes 589832 | tf_op jit(solution)/shard_map/ppermute | solution.py:317
  38.0 14.6 %collective-permute-start.3 = (bf16[128,768]{1,0:T(8,128)(2,1)S(1)}, bf16[128,768]{1,0:T(8,128)(2,1)S(1)}, u32[]{:S(2)}, u32[]{:S(2)}) collective-permute-start(bf16[128,768]{1,0:T(8,128)(2,1)S(1)} %copy-done.12), channel_id=1, source_target_pairs={{0,10},{1,15},{2,8},{3,13},{4,14},{5,11},{6,12},{7,9},{8,2},{9,7},... | collective-permute-start | bytes 589832 | tf_op jit(solution)/shard_map/ppermute | solution.py:317
  39.2 13.4 %collective-permute-start.4 = (bf16[128,768]{1,0:T(8,128)(2,1)S(1)}, bf16[128,768]{1,0:T(8,128)(2,1)S(1)}, u32[]{:S(2)}, u32[]{:S(2)}) collective-permute-start(bf16[128,768]{1,0:T(8,128)(2,1)S(1)} %copy-done.10), channel_id=1, source_target_pairs={{0,18},{1,23},{2,16},{3,21},{4,22},{5,19},{6,20},{7,17},{8,26},{9,... | collective-permute-start | bytes 589832 | tf_op jit(solution)/shard_map/ppermute | solution.py:317
  41.3 19.0 %collective-permute-start.5 = (bf16[128,768]{1,0:T(8,128)(2,1)S(1)}, bf16[128,768]{1,0:T(8,128)(2,1)S(1)}, u32[]{:S(2)}, u32[]{:S(2)}) collective-permute-start(bf16[128,768]{1,0:T(8,128)(2,1)S(1)} %copy-done.8), channel_id=1, source_target_pairs={{0,24},{1,29},{2,26},{3,31},{4,28},{5,25},{6,30},{7,27},{8,16},{9,... | collective-permute-start | bytes 589832 | tf_op jit(solution)/shard_map/ppermute | solution.py:317
  49.2 11.1 %copy-start.3 = (bf16[2,640,1024]{2,1,0:T(8,128)(2,1)S(1)}, bf16[2,640,1024]{2,1,0:T(8,128)(2,1)}, u32[]{:S(2)}) copy-start(bf16[2,640,1024]{2,1,0:T(8,128)(2,1)} %get-tuple-element.24.c_ref) | copy-start | bytes 7864324
  60.3 4.9 %copy-start.18 = (f32[512]{0:T(512)S(1)}, f32[512]{0:T(512)}, u32[]{:S(2)}) copy-start(f32[512]{0:T(512)} %param.16) | copy-start | bytes 6148
  64.5 3.0 %copy-start = (bf16[512,1024]{1,0:T(8,128)(2,1)}, bf16[512,1024]{1,0:T(8,128)(2,1)S(1)}, u32[]{:S(2)}) copy-start(bf16[512,1024]{1,0:T(8,128)(2,1)S(1)} %shard_map.123.own_ref) | copy-start | bytes 3145732
  64.5 3.0 %collective-permute-start.11 = (bf16[512,1024]{1,0:T(8,128)(2,1)S(1)}, bf16[512,1024]{1,0:T(8,128)(2,1)S(1)}, u32[]{:S(2)}, u32[]{:S(2)}) collective-permute-start(bf16[512,1024]{1,0:T(8,128)(2,1)S(1)} %shard_map.123.own_ref), channel_id=1, source_target_pairs={{0,1},{1,0},{2,3},{3,2},{4,5},{5,4},{6,7},{7,6},{8,9},{9,8},{10,11... | collective-permute-start | bytes 3145736 | tf_op jit(solution)/shard_map/ppermute | solution.py:330
  (8 other events, 7.6 us)
